TPU v7x, 128 devices: a whole 4x4x4 slice. The times are simulated.
128 devices in a mesh: row: 8 (over x, z_lo), col: 16 (over z_hi, y, core).
Axes of the slice: x: 4, y: 4, z: 4 (z_hi: 2, z_lo: 2; z = z_hi * 2 + z_lo), core: 2. Of those that a mesh axis runs over, the one named last changes fastest.
Arguments:
- slab: bfloat16 [1024, 128, 128], P(('row', 'col')), may hold values from -6 to 6
- pair: bfloat16 [1024, 1024, 128], P('row', 'col'), may hold values from -6 to 6
- mask: int32 [1024], replicated, may hold values 0 or 1
- ln_gain: float32 [128], replicated, may hold values from 0.1 to 1.9
- w_query: bfloat16 [128, 128], replicated, may hold values from -0.5 to 0.5
- w_key: bfloat16 [128, 128], replicated, may hold values from -0.5 to 0.5
- w_value: bfloat16 [128, 128], replicated, may hold values from -0.5 to 0.5
- w_gate: bfloat16 [128, 128], replicated, may hold values from -0.5 to 0.5
- gate_bias: float32 [128], replicated, may hold values from -4 to 4
- w_bias: bfloat16 [128, 4], replicated, may hold values from -24 to 24
- w_out: bfloat16 [128, 128], replicated, may hold values from -0.5 to 0.5
- out_bias: float32 [128], replicated, may hold values from -3 to 3
Outputs:
- update: bfloat16 [1024, 128, 128], P(('row', 'col'))
Inputs may be any that keep to these rules, and one draw needn't show every extreme that they name: `mask`: 1 marks a real token, 0 a padding token.
All inputs are finite; a program needn't handle non-finite values.
Results may differ from a plain program's by a relative error of at most 0.01.
The roundings to bfloat16 on the way count: a program that leaves them out, or rounds other values in their place, can miss the bound.
Values may be sent and summed in bfloat16 or wider, within the bound.
No kernel may reach another device: no remote copies, remote signals or barrier semaphores. Data moves between devices by JAX's collectives and lax.ppermute only.
A program may use at most 128 MiB of HBM per device.

v0:
```python
import math

import jax
import jax.numpy as jnp
from jax import lax
from jax.sharding import PartitionSpec as P


def in_order(pieces, dim):
    dims = list(pieces.shape[1:])
    dims[dim] *= pieces.shape[0]
    return jnp.moveaxis(pieces, 0, dim).reshape(dims)


def copy_for_each(array, axis):
    copies = jnp.broadcast_to(array, (lax.axis_size(axis), *array.shape))
    return lax.all_to_all(copies, axis, split_axis=0, concat_axis=0, tiled=True)


def gathered_copies(array, axis, dim):
    return in_order(copy_for_each(array, axis), dim)


def total_of_pieces(array, axis):
    return lax.all_gather(array, axis).max(0)


def sent_together(arrays, axis, dim, along):
    widths = [a.shape[along] for a in arrays]
    both = jnp.concatenate(arrays, axis=along)
    out = lax.psum_scatter(both, axis, scatter_dimension=dim, tiled=True)
    return tuple(jnp.split(out, [sum(widths[:k]) for k in range(1, len(widths))], axis=along))


def normalize(values, ln_gain):
    values = values.astype(jnp.float32)
    center = jnp.mean(values, axis=-1, keepdims=True)
    spread = jnp.mean(jnp.square(values - center), axis=-1, keepdims=True)
    return ((values - center) * lax.rsqrt(spread + 1e-05) * ln_gain).astype(jnp.bfloat16)


def project(rows, weight):
    flat = rows.reshape(-1, rows.shape[-1])
    result = jnp.dot(flat, weight, preferred_element_type=jnp.float32)
    return result.reshape(rows.shape[:-1] + (weight.shape[1],))


def per_device(
    slab, pair, mask, ln_gain, w_query, w_key, w_value, w_gate, gate_bias, w_bias, w_out, out_bias
):
    rows_count = lax.axis_size("row")
    cols_count = lax.axis_size("col")
    tok_blk, width, channels = slab.shape
    heads = w_bias.shape[1]
    head_dim = channels // heads
    scale = 1.0 / math.sqrt(head_dim)
    normed_pair = normalize(pair, ln_gain)
    bias_tile = jnp.einsum(
        "abc,ch->hab", normed_pair, w_bias, preferred_element_type=jnp.float32
    ).astype(jnp.bfloat16)
    mirrored = lax.all_to_all(
        lax.all_to_all(bias_tile, "col", split_axis=1, concat_axis=2, tiled=True),
        "row",
        split_axis=2,
        concat_axis=1,
        tiled=True,
    )
    col_index = lax.axis_index("col")
    mask_grid = mask.reshape(rows_count, cols_count, tok_blk)
    key_mask = lax.dynamic_index_in_dim(mask_grid, col_index, 1, keepdims=False).reshape(-1)
    key_shift = (key_mask.astype(jnp.float32) - 1.0) * 1000000000.0
    normed_own = normalize(slab, ln_gain)
    query_own = project(normed_own, w_query).astype(jnp.bfloat16)
    query_all = lax.all_gather(query_own, "col", axis=0, tiled=True)
    w_joined = jnp.concatenate([w_key, w_value], axis=1)
    joined = project(normalize(gathered_copies(slab, "row", 0), ln_gain), w_joined).astype(
        jnp.bfloat16
    )
    key_all = joined[..., :channels]
    value_all = joined[..., channels:]
    key_count = key_all.shape[0]
    query_count = query_all.shape[0]
    block_rows = math.gcd(query_count, 64)
    block_count = query_count // block_rows
    query_blocks = query_all.reshape(block_count, block_rows, width, heads, head_dim)
    bias_blocks = jnp.transpose(
        mirrored.reshape(heads, key_count, block_count, block_rows), (2, 3, 0, 1)
    )
    keys_split = key_all.reshape(key_count, width, heads, head_dim)
    values_split = value_all.reshape(key_count, width, heads, head_dim)

    def one_block(inputs):
        query_blk, bias_blk = inputs
        scores = (
            jnp.einsum("ijhd,kjhd->ihjk", query_blk, keys_split, preferred_element_type=jnp.float32)
            * scale
        )
        scores = scores + bias_blk.astype(jnp.float32)[:, :, None, :] + key_shift
        block_top = jnp.max(scores, axis=-1)
        weights = jnp.exp(scores - block_top[..., None])
        block_total = jnp.sum(weights, axis=-1)
        block_acc = jnp.einsum(
            "ihjk,kjhd->ijhd",
            weights.astype(jnp.bfloat16),
            values_split,
            preferred_element_type=jnp.float32,
        )
        return (block_top, block_total, block_acc)

    running = lax.map(one_block, (query_blocks, bias_blocks))
    local_top = running[0].reshape(query_count, heads, width)
    local_total = running[1].reshape(query_count, heads, width)
    local_acc = running[2].reshape(query_count, width, heads, head_dim)
    global_top = total_of_pieces(local_top.astype(jnp.bfloat16), "col").astype(local_top.dtype)
    rescale = jnp.exp(local_top - global_top)
    numer = (local_acc * jnp.transpose(rescale, (0, 2, 1))[..., None]).reshape(
        query_count, width, channels
    )
    denom = local_total * rescale
    numer_own, denom_own = tuple(
        (
            part.astype(jnp.float32)
            for part in sent_together(
                (numer.astype(jnp.bfloat16), denom.astype(jnp.bfloat16)), "col", 0, 1
            )
        )
    )
    attended = (
        numer_own.reshape(tok_blk, width, heads, head_dim)
        / jnp.transpose(denom_own, (0, 2, 1))[..., None]
    )
    gate = jax.nn.sigmoid(project(normed_own, w_gate) + gate_bias)
    hidden = (gate * attended.reshape(tok_blk, width, channels)).astype(jnp.bfloat16)
    update = project(hidden, w_out) + out_bias
    return update.astype(jnp.bfloat16)


def solution(mesh):
    placed = (
        P(("row", "col"), None, None),
        P("row", "col", None),
        P(),
        P(),
        P(),
        P(),
        P(),
        P(),
        P(),
        P(),
        P(),
        P(),
    )
    return jax.shard_map(
        per_device,
        mesh=mesh,
        in_specs=placed,
        out_specs=P(("row", "col"), None, None),
        check_vma=False,
    )
```

profile of v0, /device:TPU:0, one launch (start us, length us, event | category | flops | bytes accessed | tf_op | source)
XLA Modules:
  0.0 382.4 jit_solution(649589144454634105)
XLA Ops:
  6.6 1.2 convert_reduce_fusion.2
  7.8 1.3 fusion.36
  9.8 2.1 convolution_convert_fusion.1
  12.0 2.8 convert_reduce_fusion
  14.7 2.7 fusion.13
  17.5 2.9 fusion.61
  20.6 15.4 %all_to_all.38 = bf16[16,2,1024]{2,1,0:T(2,128)(2,1)S(1)} all-to-all(bf16[16,2,1024]{2,1,0:T(2,128)(2,1)S(1)} %reshape.176), channel_id=1, replica_groups=mesh['row'=8,'col'=16] {'col'}, dimensions={0} | all-to-all | bytes 131072 | tf_op jit(solution)/shard_map/all_to_all | solution.py:62
  36.2 0.7 copy.86
  36.9 1.1 reshape.178
  37.9 11.2 %all_to_all.39 = bf16[8,2,2048]{2,1,0:T(2,128)(2,1)S(1)} all-to-all(bf16[8,2,2048]{2,1,0:T(2,128)(2,1)S(1)} %reshape.178), channel_id=1, replica_groups=mesh['row'=8,'col'=16] {'row'}, dimensions={0} | all-to-all | bytes 131072 | tf_op jit(solution)/shard_map/all_to_all | solution.py:61
  49.1 1.8 broadcast_in_dim.14
  50.9 3.6 all-to-all-start
  55.0 1.2 reshape.179
  57.0 27.0 %all-to-all-done = bf16[8,8,128,128]{3,2,1,0:T(8,128)(2,1)S(1)} async-done(((bf16[8,8,128,128]{3,2,1,0:T(8,128)(2,1)}), bf16[8,8,128,128]{3,2,1,0:T(8,128)(2,1)S(1)}, u32[]{:S(2)}, u32[]{:S(2)}) %all-to-all-start) | async-done | bytes 2097184 | tf_op jit(solution)/shard_map/all_to_all | solution.py:17
  84.6 2.4 multiply_reduce_fusion
  87.0 2.5 fusion.18
  89.5 1.2 convolution_convert_fusion
  90.8 3.2 fusion.60
  94.0 3.2 copy.65
  97.2 7.6 %copy.72 = bf16[64,128,4,32]{0,3,1,2:T(8,128)(2,1)} copy(bf16[64,128,4,32]{1,3,2,0:T(8,128)(2,1)S(1)} %bitcast.117) | data formatting | bytes 4194304 | tf_op jit(solution)/shard_map/while | solution.py:110
  104.8 5.3 %copy.87 = bf16[64,128,128]{0,2,1:T(8,128)(2,1)} copy(bf16[64,128,128]{2,1,0:T(8,128)(2,1)} %get-tuple-element.115) | data formatting | bytes 4194304 | tf_op jit(solution)/shard_map/reshape | solution.py:90
  110.2 6.5 %copy.64 = bf16[128,128,128]{1,2,0:T(8,128)(2,1)} copy(bf16[128,128,128]{2,1,0:T(8,128)(2,1)} %all-gather.3.cloned.1.call-done) | data formatting | bytes 8388608 | tf_op jit(solution)/shard_map/all_gather | solution.py:74
  116.7 102.4 %while.14 = (s32[]{:T(128)}, f32[2,64,4,128]{3,1,0,2:T(8,128)S(1)}, f32[2,64,4,128]{3,2,1,0:T(4,128)S(1)}, f32[2,64,128,4,32]{2,4,3,1,0:T(8,128)}, bf16[2,64,128...) while((s32[]{:T(128)}, f32[2,64,4,128]{3,1,0,2:T(8,128)S(1)}, ...), condition=%wide.region_9.10_spmd, body=%wide.region_6.9_spmd.sunk | while | flops 289357824 | bytes 70878352 | solution.py:110
  116.7 2.0 constant_dynamic-slice_fusion.2
  118.7 7.6 %copy.126 = bf16[1,64,128,4,32]{1,4,2,3,0:T(8,128)(2,1)} copy(bf16[1,64,128,4,32]{2,4,3,1,0:T(8,128)(2,1)S(1)} %constant_dynamic-slice_fusion.2) | data formatting | bytes 4194304 | tf_op jit(solution)/shard_map/while/body/jit(dynamic_index_in_dim)/dynamic_slice | solution.py:110
  126.3 13.4 %fusion.78 = (f32[64,4,128]{0,2,1:T(8,128)S(1)}, f32[4,128,64,64]{2,3,1,0:T(8,128)}) fusion(f32[64]{0:T(128)S(1)} %get-tuple-element.211, f32[64,4,64]{0,2,1:T(8,128)S(1)} %bitcast_convert_fusion.2, bf16[64,128,4,32]{0,3,1,2:T(8,128)(2,1)} %get-tuple-element.209, bf16[1,64,128,4,32]{1,4,2,3,0:T(8,128)(2,1)} %copy.126), kind=kOutput, calls=%fused_computation.5.clone.1 | convolution fusion | flops 142573568 | bytes 12779776 | tf_op jit(solution)/shard_map/while/body/eval_jaxpr/ijhd,kjhd->ihjk/dot_general | solution.py:95
  139.7 9.6 %fusion.79 = (bf16[64,4,128,64]{0,3,2,1:T(8,128)(2,1)S(1)}, f32[64,4,128]{0,2,1:T(8,128)S(1)}) fusion(f32[4,128,64,64]{2,3,1,0:T(8,128)} %get-tuple-element.181, f32[64,4,128]{0,2,1:T(8,128)S(1)} %get-tuple-element.180, f32[64]{0:T(128)S(1)} %get-tuple-element.211, f32[64,4,64]{0,2,1:T(8,128)S(1)} %bitcast_convert_fusion.2), kind=kLoop, calls=%fused_computation.3.clone.1 | loop fusion | flops 12550144 | bytes 12910848 | tf_op jit(solution)/shard_map/while/body/eval_jaxpr/convert_element_type | solution.py:104
  149.3 4.5 %fusion.80 = f32[1,64,128,4,32]{1,4,3,2,0:T(8,128)} fusion(bf16[64,128,4,32]{0,3,2,1:T(8,128)(2,1)S(1)} %copy-done.2, bf16[64,4,128,64]{0,3,2,1:T(8,128)(2,1)S(1)} %get-tuple-element.183), kind=kOutput, calls=%fused_computation.10.clone.1 | convolution fusion | flops 134217728 | bytes 10485760 | tf_op jit(solution)/shard_map/while/body/eval_jaxpr/ihjk,kjhd->ijhd/dot_general | solution.py:102
  153.7 8.9 %copy.129 = f32[1,64,128,4,32]{2,4,3,1,0:T(8,128)} copy(f32[1,64,128,4,32]{1,4,3,2,0:T(8,128)} %fusion.80) | data formatting | bytes 8388608 | tf_op jit(solution)/shard_map/while/body/jit(dynamic_update_index_in_dim)/dynamic_update_slice | solution.py:110
  162.6 4.9 %constant_dynamic-update-slice_fusion.8 = f32[2,64,128,4,32]{2,4,3,1,0:T(8,128)} fusion(f32[2,64,128,4,32]{2,4,3,1,0:T(8,128)} %get-tuple-element.197, f32[1,64,128,4,32]{2,4,3,1,0:T(8,128)} %copy.129, s32[]{:T(128)} %get-tuple-element.194), kind=kLoop, calls=%fused_computation.12.clone.1 | loop fusion | bytes 8389120 | tf_op jit(solution)/shard_map/while/body/jit(dynamic_update_index_in_dim)/dynamic_update_slice | solution.py:110
  167.9 2.0 constant_dynamic-slice_fusion.2
  169.8 7.6 %copy.126 = bf16[1,64,128,4,32]{1,4,2,3,0:T(8,128)(2,1)} copy(bf16[1,64,128,4,32]{2,4,3,1,0:T(8,128)(2,1)S(1)} %constant_dynamic-slice_fusion.2) | data formatting | bytes 4194304 | tf_op jit(solution)/shard_map/while/body/jit(dynamic_index_in_dim)/dynamic_slice | solution.py:110
  177.4 13.4 %fusion.78 = (f32[64,4,128]{0,2,1:T(8,128)S(1)}, f32[4,128,64,64]{2,3,1,0:T(8,128)}) fusion(f32[64]{0:T(128)S(1)} %get-tuple-element.211, f32[64,4,64]{0,2,1:T(8,128)S(1)} %bitcast_convert_fusion.2, bf16[64,128,4,32]{0,3,1,2:T(8,128)(2,1)} %get-tuple-element.209, bf16[1,64,128,4,32]{1,4,2,3,0:T(8,128)(2,1)} %copy.126), kind=kOutput, calls=%fused_computation.5.clone.1 | convolution fusion | flops 142573568 | bytes 12779776 | tf_op jit(solution)/shard_map/while/body/eval_jaxpr/ijhd,kjhd->ihjk/dot_general | solution.py:95
  190.8 9.6 %fusion.79 = (bf16[64,4,128,64]{0,3,2,1:T(8,128)(2,1)S(1)}, f32[64,4,128]{0,2,1:T(8,128)S(1)}) fusion(f32[4,128,64,64]{2,3,1,0:T(8,128)} %get-tuple-element.181, f32[64,4,128]{0,2,1:T(8,128)S(1)} %get-tuple-element.180, f32[64]{0:T(128)S(1)} %get-tuple-element.211, f32[64,4,64]{0,2,1:T(8,128)S(1)} %bitcast_convert_fusion.2), kind=kLoop, calls=%fused_computation.3.clone.1 | loop fusion | flops 12550144 | bytes 12910848 | tf_op jit(solution)/shard_map/while/body/eval_jaxpr/convert_element_type | solution.py:104
  200.4 4.5 %fusion.80 = f32[1,64,128,4,32]{1,4,3,2,0:T(8,128)} fusion(bf16[64,128,4,32]{0,3,2,1:T(8,128)(2,1)S(1)} %copy-done.2, bf16[64,4,128,64]{0,3,2,1:T(8,128)(2,1)S(1)} %get-tuple-element.183), kind=kOutput, calls=%fused_computation.10.clone.1 | convolution fusion | flops 134217728 | bytes 10485760 | tf_op jit(solution)/shard_map/while/body/eval_jaxpr/ihjk,kjhd->ijhd/dot_general | solution.py:102
  204.9 8.9 %copy.129 = f32[1,64,128,4,32]{2,4,3,1,0:T(8,128)} copy(f32[1,64,128,4,32]{1,4,3,2,0:T(8,128)} %fusion.80) | data formatting | bytes 8388608 | tf_op jit(solution)/shard_map/while/body/jit(dynamic_update_index_in_dim)/dynamic_update_slice | solution.py:110
  213.8 5.0 %constant_dynamic-update-slice_fusion.8 = f32[2,64,128,4,32]{2,4,3,1,0:T(8,128)} fusion(f32[2,64,128,4,32]{2,4,3,1,0:T(8,128)} %get-tuple-element.197, f32[1,64,128,4,32]{2,4,3,1,0:T(8,128)} %copy.129, s32[]{:T(128)} %get-tuple-element.194), kind=kLoop, calls=%fused_computation.12.clone.1 | loop fusion | bytes 8389120 | tf_op jit(solution)/shard_map/while/body/jit(dynamic_update_index_in_dim)/dynamic_update_slice | solution.py:110
  219.1 0.7 convert_element_type.103
  219.8 9.3 %copy.80 = f32[128,128,128]{2,1,0:T(8,128)} copy(f32[128,128,128]{1,2,0:T(8,128)} %bitcast.118) | data formatting | bytes 16777216 | tf_op jit(solution)/shard_map/reshape | solution.py:113
  229.1 37.1 %all-gather.5.cloned.1.call-done = bf16[16,128,4,128]{3,1,2,0:T(8,128)(2,1)} async-done(((bf16[1,128,4,128]{3,1,2,0:T(8,128)(2,1)}), bf16[16,128,4,128]{3,1,2,0:T(8,128)(2,1)}) %all-gather.5.cloned.1.call-update) | async-done | bytes 2097168 | tf_op jit(solution)/shard_map/all_gather | solution.py:25
  266.2 2.0 reduce_max.18
  268.5 3.8 mul.99
  272.3 9.0 %copy.81 = f32[128,128,128]{2,1,0:T(8,128)} copy(f32[128,128,128]{1,2,0:T(8,128)} %bitcast.115) | data formatting | bytes 16777216 | tf_op jit(solution)/shard_map/mul | solution.py:116
  281.3 7.8 %multiply_convert_fusion = bf16[128,128,128]{2,1,0:T(8,128)(2,1)S(1)} fusion(f32[128,128,128]{2,1,0:T(8,128)} %copy.80, f32[128,128,128]{2,1,0:T(8,128)} %copy.81), kind=kLoop, calls=%fused_computation.16 | loop fusion | flops 4194304 | bytes 20971520 | tf_op jit(solution)/shard_map/convert_element_type | solution.py:124
  289.1 2.5 pad_maximum_fusion
  291.7 80.8 %reduce-scatter.2.cloned.1.call-done = bf16[8,132,128]{2,1,0:T(8,128)(2,1)} async-done(((bf16[128,132,128]{2,1,0:T(8,128)(2,1)}), bf16[8,132,128]{2,1,0:T(8,128)(2,1)}) %reduce-scatter.2.cloned.1.call-update) | async-done | bytes 270352 | tf_op jit(solution)/shard_map/reduce_scatter | solution.py:31
  372.6 0.7 convert_bitcast_fusion
  373.6 2.3 fusion.27
  (83 shorter events, 4.1 us)
Async XLA Ops:
  6.5 3.3 copy-start
  6.5 10.9 %copy-start.14 = (f32[128]{0:T(128)S(1)}, f32[128]{0:T(128)}, u32[]{:S(2)}) copy-start(f32[128]{0:T(128)} %param.17) | copy-start | bytes 1540
  6.5 8.2 %copy-start.3 = (bf16[128,64,128]{2,1,0:T(8,128)(2,1)S(1)}, bf16[128,64,128]{2,1,0:T(8,128)(2,1)}, u32[]{:S(2)}) copy-start(bf16[128,64,128]{2,1,0:T(8,128)(2,1)} %param.15) | copy-start | bytes 6291460
  6.5 10.9 %copy-start.18 = (bf16[128,4]{0,1:T(4,128)(2,1)S(1)}, bf16[128,4]{0,1:T(4,128)(2,1)}, u32[]{:S(2)}) copy-start(bf16[128,4]{0,1:T(4,128)(2,1)} %param.23) | copy-start | bytes 3076
  6.5 103.6 %all-gather.3.cloned.1.call-start = ((), (), s32[]{:S(2)}) async-start(), calls=%async_computation.4 | async-start | bytes 4456448 | tf_op jit(solution)/shard_map/all_gather | solution.py:74
  7.8 1.4 copy-start.9
  9.2 0.6 copy-start.12
  17.4 31.7 %copy-start.4 = (bf16[8,128,128]{2,1,0:T(8,128)(2,1)S(1)}, bf16[8,128,128]{2,1,0:T(8,128)(2,1)}, u32[]{:S(2)}) copy-start(bf16[8,128,128]{2,1,0:T(8,128)(2,1)} %param.14) | copy-start | bytes 786436
  36.9 18.0 %copy-start.11 = (s32[1024]{0:T(1024)S(1)}, s32[1024]{0:T(1024)}, u32[]{:S(2)}) copy-start(s32[1024]{0:T(1024)} %param.16) | copy-start | bytes 12292
  50.9 33.1 %all-to-all-start = ((bf16[8,8,128,128]{3,2,1,0:T(8,128)(2,1)}), bf16[8,8,128,128]{3,2,1,0:T(8,128)(2,1)S(1)}, u32[]{:S(2)}, u32[]{:S(2)}) async-start(bf16[8,8,128,128]{3,2,1,0:T(8,128)(2,1)} %broadcast_in_dim.14), calls=%async_computation | async-start | bytes 4194304 | tf_op jit(solution)/shard_map/all_to_all | solution.py:17
  54.5 211.7 %all-gather.5.cloned.1.call-start = ((), (), s32[]{:S(2)}) async-start(), calls=%async_computation.5 | async-start | bytes 2228224 | tf_op jit(solution)/shard_map/all_gather | solution.py:25
  57.0 32.5 %copy-start.7 = (bf16[128,128]{1,0:T(8,128)(2,1)S(1)}, bf16[128,128]{1,0:T(8,128)(2,1)}, u32[]{:S(2)}) copy-start(bf16[128,128]{1,0:T(8,128)(2,1)} %param.20) | copy-start | bytes 98308
  57.0 32.5 %copy-start.8 = (bf16[128,128]{1,0:T(8,128)(2,1)S(1)}, bf16[128,128]{1,0:T(8,128)(2,1)}, u32[]{:S(2)}) copy-start(bf16[128,128]{1,0:T(8,128)(2,1)} %param.19) | copy-start | bytes 98308
  110.2 6.5 %copy-start.6 = (f32[2,64,4,128]{3,2,1,0:T(4,128)S(1)}, f32[2,64,4,128]{3,2,1,0:T(4,128)}, u32[]{:S(2)}) copy-start(f32[2,64,4,128]{3,2,1,0:T(4,128)} %custom-call.1) | copy-start | bytes 786436
  139.7 9.6 %copy-start.2 = (bf16[64,128,4,32]{0,3,2,1:T(8,128)(2,1)S(1)}, bf16[64,128,4,32]{0,3,2,1:T(8,128)(2,1)}, u32[]{:S(2)}) copy-start(bf16[64,128,4,32]{0,3,2,1:T(8,128)(2,1)} %get-tuple-element.212) | copy-start | bytes 6291460 | tf_op jit(solution)/shard_map/while
  190.8 9.6 %copy-start.2 = (bf16[64,128,4,32]{0,3,2,1:T(8,128)(2,1)S(1)}, bf16[64,128,4,32]{0,3,2,1:T(8,128)(2,1)}, u32[]{:S(2)}) copy-start(bf16[64,128,4,32]{0,3,2,1:T(8,128)(2,1)} %get-tuple-element.212) | copy-start | bytes 6291460 | tf_op jit(solution)/shard_map/while
  219.8 152.8 %reduce-scatter.2.cloned.1.call-start = ((), (), s32[]{:S(2)}) async-start(), calls=%async_computation.6 | async-start | bytes 4734976 | tf_op jit(solution)/shard_map/reduce_scatter | solution.py:31
  291.6 81.9 %copy-start.5 = (bf16[8,128,128]{2,1,0:T(8,128)(2,1)S(1)}, bf16[8,128,128]{2,1,0:T(8,128)(2,1)}, u32[]{:S(2)}) copy-start(bf16[8,128,128]{2,1,0:T(8,128)(2,1)} %param.14) | copy-start | bytes 786436
  291.6 81.9 %copy-start.10 = (f32[8,128]{1,0:T(8,128)S(1)}, f32[8,128]{1,0:T(8,128)}, u32[]{:S(2)}) copy-start(f32[8,128]{1,0:T(8,128)} %copy-done.9) | copy-start | bytes 12292
  291.6 81.9 %copy-start.13 = (f32[8,128]{1,0:T(8,128)S(1)}, f32[8,128]{1,0:T(8,128)}, u32[]{:S(2)}) copy-start(f32[8,128]{1,0:T(8,128)} %copy-done.12) | copy-start | bytes 12292
  291.6 81.9 %copy-start.15 = (f32[128]{0:T(128)S(1)}, f32[128]{0:T(128)}, u32[]{:S(2)}) copy-start(f32[128]{0:T(128)} %param.17) | copy-start | bytes 1540
  291.6 81.9 %copy-start.16 = (bf16[128,128]{1,0:T(8,128)(2,1)S(1)}, bf16[128,128]{1,0:T(8,128)(2,1)}, u32[]{:S(2)}) copy-start(bf16[128,128]{1,0:T(8,128)(2,1)} %param.24) | copy-start | bytes 98308
  291.7 81.9 %copy-start.17 = (bf16[128,128]{1,0:T(8,128)(2,1)S(1)}, bf16[128,128]{1,0:T(8,128)(2,1)}, u32[]{:S(2)}) copy-start(bf16[128,128]{1,0:T(8,128)(2,1)} %param.21) | copy-start | bytes 98308
  291.7 81.9 %copy-start.19 = (f32[128]{0:T(128)S(1)}, f32[128]{0:T(128)}, u32[]{:S(2)}) copy-start(f32[128]{0:T(128)} %param.25) | copy-start | bytes 1540
  291.7 81.9 %copy-start.20 = (f32[128]{0:T(128)S(1)}, f32[128]{0:T(128)}, u32[]{:S(2)}) copy-start(f32[128]{0:T(128)} %param.22) | copy-start | bytes 1540
  291.7 84.2 %copy-start.1 = (bf16[128,128]{1,0:T(8,128)(2,1)S(1)}, bf16[128,128]{1,0:T(8,128)(2,1)}, u32[]{:S(2)}) copy-start(bf16[128,128]{1,0:T(8,128)(2,1)} %param.18) | copy-start | bytes 98308
Sparse Core Ops, SparseCore 0:
  12.1 81.0 all-gather.2
  219.9 46.2 all-gather.4
  291.8 80.6 reduce-scatter.1
where the time goes:
time: 384 us; the launch traced here: 382 us
  waiting for transfers between devices  145 us (38%)
  local copies, waits for them, and re-layouts  102 us (27%)
  other arithmetic  46.8 us (12%)
  matrix products  44.3 us (12%)
  blocking collectives  26.6 us (7%)
  between operations  13.6 us (4%)
  starting transfers between devices  3.9 us (1%)
    reduce_scatter x1, waiting for transfers between devices, sent_together(): out = lax.psum_scatter(both, axis, scatter_dimension=dim, tiled=True)  80.8 us
    all_gather x1, waiting for transfers between devices, total_of_pieces(): return lax.all_gather(array, axis).max(0)  37.1 us
    dynamic_update_slice x12, local copies, waits for them, and re-layouts, per_device(): running = lax.map(one_block, (query_blocks, bias_blocks))  28.2 us
    all_to_all x1, waiting for transfers between devices, copy_for_each(): return lax.all_to_all(copies, axis, split_axis=0, concat_axis=0, tiled=True)  27 us
    dot_general x2, matrix products, one_block(): jnp.einsum('ijhd,kjhd->ihjk', query_blk, keys_split, preferred_element_ty...  26.8 us
    dynamic_slice x4, local copies, waits for them, and re-layouts, per_device(): running = lax.map(one_block, (query_blocks, bias_blocks))  19.2 us
    convert_element_type x2, other arithmetic, one_block(): weights.astype(jnp.bfloat16)  19.2 us
    all_to_all x1, blocking collectives, per_device(): lax.all_to_all(bias_tile, 'col', split_axis=1, concat_axis=2, tiled=True)  15.4 us
  transfers between devices with their start and end apart: 4, of which 3 were waited for; matrix products, arithmetic and copies ran while one was open for 13% of the time, Pallas kernels for 0%

commit v1 on v0

v1 whole, which is shorter than its diff:
```python
import functools
import math

import jax
import jax.numpy as jnp
from jax import lax
from jax.experimental import pallas as pl
from jax.experimental.pallas import tpu as pltpu
from jax.sharding import Mesh
from jax.sharding import PartitionSpec as P

F32 = jnp.float32
BF16 = jnp.bfloat16
LOG2E = math.log2(math.e)

AXES = ("x", "zl", "zh", "y", "c")
SIZES = (4, 2, 2, 4, 2)
GROUP = ("x", "zl", "zh")
NG = 16
NB = 8
TB = 8
HEADS = 4
HALF = 4


def layer_norm(x, gain):
    center = jnp.mean(x, axis=-1, keepdims=True)
    d = x - center
    spread = jnp.mean(d * d, axis=-1, keepdims=True)
    return d * lax.rsqrt(spread + 1e-5) * gain


def pack_kernel(slab_ref, pair_ref, gain_ref, wb_ref, out_ref, nslab, npair, rows):
    b = pl.program_id(0)
    gain = gain_ref[...]

    @pl.when(b == 0)
    def _():
        nslab[...] = layer_norm(slab_ref[...].astype(F32).reshape(1024, 128), gain)

    npair[...] = layer_norm(pair_ref[...].astype(F32).reshape(1024, 128), gain)
    wb = wb_ref[...]
    for i in range(TB):
        x = npair[pl.ds(i, 128, stride=TB), :].astype(BF16)
        t = lax.dot_general(wb, x, (((1,), (1,)), ((), ())), preferred_element_type=F32)
        rows[pl.ds(i, TB, stride=TB), :] = t
    bias = rows[0 : HEADS * TB, :].reshape(HEADS, TB, 128).astype(BF16)
    half = (b % 2) * HALF
    for g in range(NG):
        out_ref[g, 0, HALF : HALF + HEADS] = bias
        for j in range(HALF):
            out_ref[g, 0, j] = nslab[pl.ds(half + (g * 8 + j), TB, stride=128), :].astype(BF16)


def attend_kernel(
    idx_ref, recv_ref, other_ref, mask_ref, wkv_ref, wqg_ref, wo_ref, gb_ref, ob_ref,
    out_ref, bias, kbuf, vbuf, qbuf, gate, upd,
):
    b = idx_ref[0]
    core = idx_ref[1]
    for r in range(8):
        shift = (mask_ref[r : r + 1, :].astype(F32) - 1.0) * 1e9
        for h in range(HEADS):
            tile = recv_ref[2 * r : 2 * r + 2, :, HALF + h].astype(F32).reshape(128, 128)
            bias[h * 128 : (h + 1) * 128, r * 128 : (r + 1) * 128] = (tile + shift) * LOG2E

    wkv = wkv_ref[...]
    wqg = wqg_ref[...]
    gb = gb_ref[...]

    def project(src, half):
        def step(j, _):
            col = half * HALF + j
            x = src[:, :, j].astype(F32).reshape(1024, 128).astype(BF16)
            kv = jnp.dot(x, wkv, preferred_element_type=F32)
            kbuf[col] = kv[:, :128].astype(BF16)
            vbuf[col] = kv[:, 128:].astype(BF16)
            xq = src[:, b, j].astype(F32).reshape(128, 128).astype(BF16)
            qg = jnp.dot(xq, wqg, preferred_element_type=F32)
            qbuf[col] = qg[:, :128].astype(BF16)
            gate[col] = jax.nn.sigmoid(qg[:, 128:] + gb)
            return 0

        lax.fori_loop(0, HALF, step, 0)

    project(recv_ref, core)
    project(other_ref, 1 - core)

    lane_head = lax.broadcasted_iota(jnp.int32, (128, 128), 1) // 32
    wo = wo_ref[...]
    ob = ob_ref[...]

    def attend(col, _):
        k = kbuf[col]
        v = vbuf[col]
        q = qbuf[col].astype(F32)
        att = jnp.zeros((128, 128), F32)
        for h in range(HEADS):
            qh = jnp.where(lane_head == h, q, 0.0).astype(BF16)
            s = lax.dot_general(qh, k, (((1,), (1,)), ((), ())), preferred_element_type=F32)
            s = s * (LOG2E / math.sqrt(32.0)) + bias[h * 128 : (h + 1) * 128, :]
            p = jnp.exp2(s - jnp.max(s, axis=-1, keepdims=True))
            total = jnp.sum(p, axis=-1, keepdims=True)
            o = jnp.dot(p.astype(BF16), v, preferred_element_type=F32)
            att = jnp.where(lane_head == h, o * (1.0 / total), att)
        hidden = (gate[col] * att).astype(BF16)
        upd[pl.ds(col, 128, stride=8), :] = jnp.dot(hidden, wo, preferred_element_type=F32) + ob
        return 0

    lax.fori_loop(0, 2 * HALF, attend, 0)
    out_ref[...] = upd[...].reshape(16, 8, 8, 128).astype(BF16)


def pack(slab, pair, gain, wb):
    return pl.pallas_call(
        pack_kernel,
        grid=(NB,),
        in_specs=[
            pl.BlockSpec((8, 128, 128), lambda b: (0, 0, 0)),
            pl.BlockSpec((128, TB, 128), lambda b: (0, b, 0)),
            pl.BlockSpec((1, 128), lambda b: (0, 0)),
            pl.BlockSpec((8, 128), lambda b: (0, 0)),
        ],
        out_specs=pl.BlockSpec((NG, 1, 8, TB, 128), lambda b: (0, b, 0, 0, 0)),
        out_shape=jax.ShapeDtypeStruct((NG, NB, 8, TB, 128), BF16),
        scratch_shapes=[
            pltpu.VMEM((1024, 128), F32),
            pltpu.VMEM((1024, 128), F32),
            pltpu.VMEM((64, 128), F32),
        ],
        name="pack",
    )(slab, pair, gain, wb)


def attend(idx, recv, other, mask, wkv, wqg, wo, gb, ob):
    smem = pl.BlockSpec(memory_space=pltpu.SMEM)
    vmem = pl.BlockSpec(memory_space=pltpu.VMEM)
    return pl.pallas_call(
        attend_kernel,
        in_specs=[smem] + [vmem] * 8,
        out_specs=vmem,
        out_shape=jax.ShapeDtypeStruct((16, TB, 8, 128), BF16),
        scratch_shapes=[
            pltpu.VMEM((512, 1024), F32),
            pltpu.VMEM((8, 1024, 128), BF16),
            pltpu.VMEM((8, 1024, 128), BF16),
            pltpu.VMEM((8, 128, 128), BF16),
            pltpu.VMEM((8, 128, 128), F32),
            pltpu.VMEM((1024, 128), F32),
        ],
        name="attend",
    )(idx, recv, other, mask, wkv, wqg, wo, gb, ob)


def per_device(
    slab, pair, mask, ln_gain, w_query, w_key, w_value, w_gate, gate_bias, w_bias, w_out, out_bias
):
    core = lax.axis_index("c")
    b = lax.axis_index("y") * 2 + core
    wb = jnp.pad(w_bias.T, ((0, 8 - HEADS), (0, 0)))
    packed = pack(slab, pair, ln_gain.reshape(1, 128), wb)
    recv = lax.all_to_all(
        packed.reshape(NG * NB, 8, TB, 128), AXES, split_axis=0, concat_axis=0, tiled=True
    ).reshape(NG, NB, 8, TB, 128)
    other = lax.ppermute(recv[:, :, :HALF], "c", [(0, 1), (1, 0)])
    update = attend(
        jnp.stack([b, core]).astype(jnp.int32),
        recv,
        other,
        mask.reshape(8, 128),
        jnp.concatenate([w_key, w_value], axis=1),
        jnp.concatenate([w_query, w_gate], axis=1),
        w_out,
        gate_bias.reshape(1, 128),
        out_bias.reshape(1, 128),
    )
    home = lax.all_to_all(update, GROUP, split_axis=0, concat_axis=0, tiled=True)
    return jnp.transpose(home, (1, 0, 2, 3)).reshape(8, 128, 128)


def solution(mesh):
    fine = Mesh(mesh.devices.reshape(SIZES), AXES)
    whole = P(AXES, None, None)
    placed = (whole, P(("x", "zl"), ("zh", "y", "c"), None)) + (P(),) * 10
    return jax.shard_map(
        per_device, mesh=fine, in_specs=placed, out_specs=whole, check_vma=False
    )
```

time: 384 us -> 89.4 us (0.23)
  waiting for transfers between devices: 145 us -> 1.6 us
  local copies, waits for them, and re-layouts: 102 us -> 4.12 us
  other arithmetic: 46.8 us -> 1.25 us
  matrix products: 44.3 us -> 0 us
  Pallas kernels: 0 us -> 27.7 us
  blocking collectives: 26.6 us -> 54.2 us
  between operations: 13.6 us -> 0.03 us
  starting transfers between devices: 3.9 us -> 0.01 us
    reduce_scatter x1 -> x0, waiting for transfers between devices: 80.8 us -> none  [sent_together(): out = lax.psum_scatter(both, axis, scatter_dimension=dim, tiled=True)]
    dot_general x8 -> x0, matrix products: 44.3 us -> none  [the longest x2 26.8 us: one_block(): jnp.einsum('ijhd,kjhd->ihjk', query_blk, keys_split, preferred_element_ty...]
    all_gather x2 -> x0, waiting for transfers between devices: 37.1 us -> none  [the longest x1 37.1 us: total_of_pieces(): return lax.all_gather(array, axis).max(0)]
    convert_element_type x7 -> x0, other arithmetic: 30.1 us -> none  [the longest x2 19.2 us: one_block(): weights.astype(jnp.bfloat16)]
    dynamic_update_slice x12 -> x0, local copies, waits for them, and re-layouts: 28.2 us -> none  [per_device(): running = lax.map(one_block, (query_blocks, bias_blocks))]
    pallas_call x0 -> x2, Pallas kernels: none -> 27.7 us  [the longest x1 18.9 us: attend(): pl.pallas_call(attend_kernel, in_specs=[smem] + [vmem] * 8, out_specs=vme...]
    all_to_all x2, blocking collectives: 26.6 us -> 54.2 us  [the longest x1 41.4 us: per_device(): lax.all_to_all(packed.reshape(NG * NB, 8, TB, 128), AXES, split_axis=0, c...]
    all_to_all x1 -> x0, waiting for transfers between devices: 27 us -> none  [copy_for_each(): return lax.all_to_all(copies, axis, split_axis=0, concat_axis=0, tiled=True)]
  transfers between devices with their start and end apart: 4 -> 1, of which waited for: 3 -> 1; matrix products, arithmetic and copies ran while one was open for 13% -> 1% of each run, Pallas kernels for 0% -> 0%
where the time goes in v1:
time: 89.4 us; the launch traced here: 88.9 us
  blocking collectives  54.2 us (61%)
  Pallas kernels  27.7 us (31%)
  local copies, waits for them, and re-layouts  4.12 us (5%)
  waiting for transfers between devices  1.6 us (2%)
  other arithmetic  1.25 us (1%)
    all_to_all x1, blocking collectives, per_device(): lax.all_to_all(packed.reshape(NG * NB, 8, TB, 128), AXES, split_axis=0, c...  41.4 us
    pallas_call x1, Pallas kernels, attend(): pl.pallas_call(attend_kernel, in_specs=[smem] + [vmem] * 8, out_specs=vme...  18.9 us
    all_to_all x1, blocking collectives, per_device(): lax.all_to_all(update, GROUP, split_axis=0, concat_axis=0, tiled=True)  12.8 us
    pallas_call x1, Pallas kernels, pack(): pl.pallas_call(pack_kernel, grid=(NB,), in_specs=[pl.BlockSpec((8, 128, 1...  8.85 us
  transfers between devices with their start and end apart: 1, of which 1 were waited for; matrix products, arithmetic and copies ran while one was open for 1% of the time, Pallas kernels for 0%

profile of v1, /device:TPU:0, one launch (start us, length us, event | category | flops | bytes accessed | tf_op | source)
XLA Modules:
  0.0 88.9 jit_solution(17751808563310955342)
XLA Ops:
  0.0 1.3 %pad.4.wb_ref = bf16[8,128]{1,0:T(8,128)(2,1)} pad(bf16[4,128]{1,0:T(4,128)(2,1)} %bitcast.18, bf16[]{:T(256)} %constant.12.clone.1), padding=0_4x0_0 | pad | bytes 3074 | tf_op jit(solution)/shard_map/jit(_pad)/pad | solution.py:160
  1.3 8.8 %pack.1 = bf16[16,8,8,8,128]{4,3,2,1,0:T(8,128)(2,1)} custom-call(bf16[8,128,128]{2,1,0:T(8,128)(2,1)} %slab_ref.1, bf16[128,64,128]{2,1,0:T(8,128)(2,1)} %pair_ref.1, f32[1,128]{1,0:T(1,128)} %bitcast.19, bf16[8,128]{1,0:T(8,128)(2,1)} %pad.4.wb_ref), custom_call_target="tpu_custom_call" | custom-call | tf_op jit(solution)/shard_map/pack/pallas_call | solution.py:115
  10.1 41.4 %all_to_all.10 = bf16[128,8,8,128]{3,2,1,0:T(8,128)(2,1)S(1)} all-to-all(bf16[128,8,8,128]{3,2,1,0:T(8,128)(2,1)} %bitcast.16), channel_id=1, replica_groups=mesh['x'=4,'zl'=2,'zh'=2,'y'=4,'c'=2] {'x','zl','zh','y','c'}, dimensions={0} | all-to-all | bytes 4194304 | tf_op jit(solution)/shard_map/all_to_all | solution.py:162
  51.5 0.0 copy-start
  51.5 0.0 copy-start.2
  51.5 0.0 copy-start.3
  51.5 0.0 copy-start.4
  51.5 0.0 copy-start.5
  51.5 1.1 %slice.4 = bf16[16,8,4,8,128]{4,3,2,1,0:T(8,128)(2,1)} slice(bf16[16,8,8,8,128]{4,3,2,1,0:T(8,128)(2,1)S(1)} %bitcast.14), slice={[0:16], [0:8], [0:4], [0:8], [0:128]} | slice | bytes 2097152 | tf_op jit(solution)/shard_map/slice | solution.py:165
  52.6 0.0 collective-permute-start
  52.6 0.6 pad_add_fusion.idx_ref
  53.2 0.0 copy-done.2
  53.2 0.0 copy-done.3
  53.2 0.0 copy-done.4
  53.2 0.0 copy-done.5
  53.2 0.7 pad_maximum_fusion
  53.9 1.6 %collective-permute-done.other_ref = bf16[16,8,4,8,128]{4,3,2,1,0:T(8,128)(2,1)S(1)} collective-permute-done((bf16[16,8,4,8,128]{4,3,2,1,0:T(8,128)(2,1)}, bf16[16,8,4,8,128]{4,3,2,1,0:T(8,128)(2,1)S(1)}, u32[]{:S(2)}, u32[]{:S(2)}) %collective-permute-start) | collective-permute-done | bytes 1048608 | tf_op jit(solution)/shard_map/ppermute | solution.py:165
  55.5 0.0 copy-start.1
  55.5 0.0 copy-done
  55.5 1.0 %copy-done.1 = bf16[16,8,4,8,128]{4,3,2,1,0:T(8,128)(2,1)} copy-done((bf16[16,8,4,8,128]{4,3,2,1,0:T(8,128)(2,1)}, bf16[16,8,4,8,128]{4,3,2,1,0:T(8,128)(2,1)S(1)}, u32[]{:S(2)}) %copy-start.1) | copy-done | bytes 1048600
  56.5 18.9 %attend.1 = bf16[16,8,8,128]{3,2,1,0:T(8,128)(2,1)} custom-call(s32[2]{0:T(128)} %pad_add_fusion.idx_ref, bf16[16,8,8,8,128]{4,3,2,1,0:T(8,128)(2,1)} %bitcast.15, bf16[16,8,4,8,128]{4,3,2,1,0:T(8,128)(2,1)} %copy-done.1, s32[8,128]{1,0:T(8,128)} %bitcast.17, bf16[128,256]{1,0:T(8,128)(2,1)} %get-tuple-element.5.wkv_ref, ...), custom_call_target="tpu_custom_call" | custom-call | tf_op jit(solution)/shard_map/attend/pallas_call | solution.py:138
  75.3 12.8 %all_to_all.11 = bf16[16,8,8,128]{3,2,1,0:T(8,128)(2,1)S(1)} all-to-all(bf16[16,8,8,128]{3,2,1,0:T(8,128)(2,1)} %attend.1), channel_id=1, replica_groups=mesh['x'=4,'zl'=2,'zh'=2,'y'=4,'c'=2] {'x','zl','zh'}, dimensions={0} | all-to-all | bytes 524288 | tf_op jit(solution)/shard_map/all_to_all | solution.py:177
  88.2 0.8 copy_bitcast_fusion
Async XLA Ops:
  51.5 4.0 %copy-start = (bf16[128,8,8,128]{3,2,1,0:T(8,128)(2,1)}, bf16[128,8,8,128]{3,2,1,0:T(8,128)(2,1)S(1)}, u32[]{:S(2)}) copy-start(bf16[128,8,8,128]{3,2,1,0:T(8,128)(2,1)S(1)} %all_to_all.10) | copy-start | bytes 6291460
  51.5 1.7 %copy-start.2 = (bf16[128,128]{1,0:T(8,128)(2,1)S(1)}, bf16[128,128]{1,0:T(8,128)(2,1)}, u32[]{:S(2)}) copy-start(bf16[128,128]{1,0:T(8,128)(2,1)} %param.18) | copy-start | bytes 98308
  51.5 1.7 %copy-start.3 = (bf16[128,128]{1,0:T(8,128)(2,1)S(1)}, bf16[128,128]{1,0:T(8,128)(2,1)}, u32[]{:S(2)}) copy-start(bf16[128,128]{1,0:T(8,128)(2,1)} %param.17) | copy-start | bytes 98308
  51.5 1.7 %copy-start.4 = (bf16[128,128]{1,0:T(8,128)(2,1)S(1)}, bf16[128,128]{1,0:T(8,128)(2,1)}, u32[]{:S(2)}) copy-start(bf16[128,128]{1,0:T(8,128)(2,1)} %param.19) | copy-start | bytes 98308
  51.5 1.7 %copy-start.5 = (bf16[128,128]{1,0:T(8,128)(2,1)S(1)}, bf16[128,128]{1,0:T(8,128)(2,1)}, u32[]{:S(2)}) copy-start(bf16[128,128]{1,0:T(8,128)(2,1)} %param.16) | copy-start | bytes 98308
  52.6 2.9 %collective-permute-start = (bf16[16,8,4,8,128]{4,3,2,1,0:T(8,128)(2,1)}, bf16[16,8,4,8,128]{4,3,2,1,0:T(8,128)(2,1)S(1)}, u32[]{:S(2)}, u32[]{:S(2)}) collective-permute-start(bf16[16,8,4,8,128]{4,3,2,1,0:T(8,128)(2,1)} %slice.4), channel_id=1, source_target_pairs={{0,1},{1,0},{2,3},{3,2},{4,5},{5,4},{6,7},{7,6},{8,9},{9,8},{10,11... | collective-permute-start | bytes 3145736 | tf_op jit(solution)/shard_map/ppermute | solution.py:165
  55.5 1.0 %copy-start.1 = (bf16[16,8,4,8,128]{4,3,2,1,0:T(8,128)(2,1)}, bf16[16,8,4,8,128]{4,3,2,1,0:T(8,128)(2,1)S(1)}, u32[]{:S(2)}) copy-start(bf16[16,8,4,8,128]{4,3,2,1,0:T(8,128)(2,1)S(1)} %collective-permute-done.other_ref) | copy-start | bytes 3145732

commit v2 on v1

v2 whole, which is shorter than its diff:
```python
import math

import jax
import jax.numpy as jnp
from jax import lax
from jax.experimental import pallas as pl
from jax.experimental.pallas import tpu as pltpu
from jax.sharding import Mesh
from jax.sharding import PartitionSpec as P

F32 = jnp.float32
BF16 = jnp.bfloat16
LOG2E = math.log2(math.e)

AXES = ("x", "zl", "zh", "y", "c")
SIZES = (4, 2, 2, 4, 2)
GROUP = ("x", "zl", "zh")
NG = 16
NB = 8
TB = 8
HEADS = 4
HALF = 4
COLS = 8
CHUNK = 16

VMEM = pl.BlockSpec(memory_space=pltpu.VMEM)
ANY = pl.BlockSpec(memory_space=pl.ANY)


def pack_kernel(
    slab_ref, pair_ref, gain_ref, wb_ref,
    out_ref, pbuf, nslab, npair, rows, pslab, pbias, in_sem, slab_sem, bias_sem,
):
    loads = [
        pltpu.make_async_copy(pair_ref.at[pl.ds(16 * n, 16)], pbuf.at[pl.ds(16 * n, 16)], in_sem.at[n])
        for n in range(8)
    ]
    for load in loads:
        load.start()
    ones = jnp.full((128, 128), 1.0 / 128, BF16)
    gain = gain_ref[...]
    wb = wb_ref[...]

    def norm(x):
        d = x.astype(F32) - jnp.dot(x, ones, preferred_element_type=F32)
        spread = jnp.mean(d * d, axis=-1, keepdims=True)
        return d * lax.rsqrt(spread + 1e-5) * gain

    nslab[...] = norm(slab_ref[...].reshape(1024, 128))
    for col in range(128):
        piece = nslab[pl.ds(col, TB, stride=128), :].astype(BF16)
        pslab[col // COLS, col % COLS // HALF, col % HALF] = piece
    stores = [
        pltpu.make_async_copy(pslab, out_ref.at[:, pl.ds(2 * y, 2), pl.ds(0, HALF)], slab_sem.at[y])
        for y in range(4)
    ]
    for store in stores:
        store.start()
    for n in range(8):
        loads[n].wait()
        x = norm(pbuf[16 * n : 16 * n + 16].reshape(1024, 128))
        for k in range(16):
            for b in range(NB):
                at = 1024 * b + TB * (16 * n + k)
                npair[at : at + TB, :] = x[64 * k + TB * b : 64 * k + TB * b + TB]
    for b in range(NB):
        for i in range(TB):
            x = npair[pl.ds(1024 * b + i, 128, stride=TB), :].astype(BF16)
            t = lax.dot_general(wb, x, (((1,), (1,)), ((), ())), preferred_element_type=F32)
            rows[pl.ds(HEADS * TB * b + i, HEADS, stride=TB), :] = t
    pbias[...] = rows[...].reshape(NB, HEADS, TB, 128).astype(BF16)
    more = [
        pltpu.make_async_copy(pbias, out_ref.at[g, :, pl.ds(HALF, HEADS)], bias_sem.at[g])
        for g in range(NG)
    ]
    for store in more:
        store.start()
    for store in stores + more:
        store.wait()


def pack(slab, pair, gain, wb):
    return pl.pallas_call(
        pack_kernel,
        in_specs=[VMEM, ANY, VMEM, VMEM],
        out_specs=ANY,
        out_shape=jax.ShapeDtypeStruct((NG, NB, HALF + HEADS, TB, 128), BF16),
        scratch_shapes=[
            pltpu.VMEM((128, 64, 128), BF16),
            pltpu.VMEM((1024, 128), F32),
            pltpu.VMEM((8192, 128), F32),
            pltpu.VMEM((NB * HEADS * TB, 128), F32),
            pltpu.VMEM((NG, 2, HALF, TB, 128), BF16),
            pltpu.VMEM((NB, HEADS, TB, 128), BF16),
            pltpu.SemaphoreType.DMA((8,)),
            pltpu.SemaphoreType.DMA((4,)),
            pltpu.SemaphoreType.DMA((NG,)),
        ],
        name="pack",
    )(slab, pair, gain, wb)


def attend_kernel(
    own_ref, other_ref, tiles_ref, mask_ref, wk_ref, wv_ref, wq_ref, wg_ref, gb_ref, wo_ref, ob_ref,
    out_ref, bias, s_even, s_odd, v_even, v_odd, g_even, g_odd, weights, inverse, product, upd,
):
    step = pl.program_id(0)
    core = lax.axis_index("c")
    b = 2 * lax.axis_index("y") + core

    @pl.when(step == 0)
    def _():
        for r in range(8):
            shift = (mask_ref[r : r + 1, :].astype(F32) - 1.0) * 1e9
            for h in range(HEADS):
                tile = tiles_ref[2 * r : 2 * r + 2, :, h].astype(F32).reshape(128, 128)
                bias[h * 128 : (h + 1) * 128, r * 128 : (r + 1) * 128] = (tile + shift) * LOG2E

    lane_head = lax.broadcasted_iota(jnp.int32, (128, 128), 1) // 32
    mine = step < HALF

    def pick(own, other):
        return jnp.where(mine, own.astype(F32), other.astype(F32))

    def queries(gate):
        xq = pick(own_ref[:, b, 0], other_ref[:, b, 0]).reshape(128, 128).astype(BF16)
        wqg = jnp.concatenate([wq_ref[...], wg_ref[...]], axis=1)
        qg = jnp.dot(xq, wqg, preferred_element_type=F32)
        gate[...] = jax.nn.sigmoid(qg[:, 128:] + gb_ref[...])
        q = qg[:, :128].astype(BF16).astype(F32)
        return jnp.concatenate(
            [jnp.where(lane_head == h, q, 0.0).astype(BF16) for h in range(HEADS)], axis=0
        )

    def scores(n, q, new, value):
        at = slice(n * 4, n * 4 + 4)
        keys = slice(n * 256, n * 256 + 256)
        x = pick(own_ref[at, :, 0], other_ref[at, :, 0]).reshape(256, 128).astype(BF16)
        wkv = jnp.concatenate([wk_ref[...], wv_ref[...]], axis=1)
        kv = jnp.dot(x, wkv, preferred_element_type=F32)
        value[keys, :] = kv[:, 128:].astype(BF16)
        s = lax.dot_general(
            q, kv[:, :128].astype(BF16), (((1,), (1,)), ((), ())), preferred_element_type=F32
        )
        new[:, keys] = s * (LOG2E / math.sqrt(32.0)) + bias[:, keys]

    def softmax(n, old):
        for m in range(n * 128, n * 128 + 128, CHUNK):
            at = slice(m, m + CHUNK)
            s = old[at, :]
            p = jnp.exp2(s - jnp.max(s, axis=-1, keepdims=True))
            total = jnp.sum(p, axis=-1, keepdims=True)
            weights[at, :] = p.astype(BF16)
            inverse[at, :] = jnp.broadcast_to(1.0 / total, (CHUNK, 128))

    def products(n, value):
        at = slice(n * 256, n * 256 + 256)
        o = jnp.dot(weights[at, :], value[...], preferred_element_type=F32)
        product[at, :] = o * inverse[at, :]

    def finish(gate):
        att = product[0:128]
        for h in range(1, HEADS):
            att = jnp.where(lane_head == h, product[h * 128 : (h + 1) * 128], att)
        hidden = (gate[...] * att).astype(BF16)
        u = jnp.dot(hidden, wo_ref[...], preferred_element_type=F32) + ob_ref[...]
        before = step - 1
        col = jnp.where(before < HALF, before + core * HALF, before - core * HALF)
        upd[pl.ds(col, 128, stride=COLS), :] = u

    def body(new, old):
        if new is not None:
            q = queries(new[2])
        for n in range(4):
            if new is not None:
                scores(n, q, new[0], new[1])
            if old is not None:
                softmax(n, old[0])
                if n % 2:
                    products(n // 2, old[1])
        if old is not None:
            finish(old[2])

    even = (s_even, v_even, g_even)
    odd = (s_odd, v_odd, g_odd)

    @pl.when(step == 0)
    def _():
        body(even, None)

    @pl.when((step % 2 == 0) & (step > 0) & (step < COLS))
    def _():
        body(even, odd)

    @pl.when(step % 2 == 1)
    def _():
        body(odd, even)

    @pl.when(step == COLS)
    def _():
        body(None, odd)
        out_ref[...] = upd[...].reshape(16, TB, COLS, 128).astype(BF16)


def attend(recv, other, mask, wk, wv, wq, wg, gb, wo, ob):
    const = lambda s: (0, 0)
    column = (NG, NB, 1, TB, 128)
    square = pl.BlockSpec((128, 128), const)
    line = pl.BlockSpec((1, 128), const)
    return pl.pallas_call(
        attend_kernel,
        grid=(COLS + 1,),
        in_specs=[
            pl.BlockSpec(column, lambda s: (0, 0, jnp.minimum(s, HALF - 1), 0, 0)),
            pl.BlockSpec(column, lambda s: (0, 0, jnp.clip(s - HALF, 0, HALF - 1), 0, 0)),
            pl.BlockSpec((NG, NB, HEADS, TB, 128), lambda s: (0, 0, 1, 0, 0)),
            pl.BlockSpec((8, 128), const),
            square,
            square,
            square,
            square,
            line,
            square,
            line,
        ],
        out_specs=pl.BlockSpec((NG, TB, COLS, 128), lambda s: (0, 0, 0, 0)),
        out_shape=jax.ShapeDtypeStruct((NG, TB, COLS, 128), BF16),
        scratch_shapes=[
            pltpu.VMEM((512, 1024), F32),
            pltpu.VMEM((512, 1024), F32),
            pltpu.VMEM((512, 1024), F32),
            pltpu.VMEM((1024, 128), BF16),
            pltpu.VMEM((1024, 128), BF16),
            pltpu.VMEM((128, 128), F32),
            pltpu.VMEM((128, 128), F32),
            pltpu.VMEM((512, 1024), BF16),
            pltpu.VMEM((512, 128), F32),
            pltpu.VMEM((512, 128), F32),
            pltpu.VMEM((1024, 128), F32),
        ],
        name="attend",
    )(recv, other, recv, mask, wk, wv, wq, wg, gb, wo, ob)


def per_device(
    slab, pair, mask, ln_gain, w_query, w_key, w_value, w_gate, gate_bias, w_bias, w_out, out_bias
):
    packed = pack(slab, pair, ln_gain.reshape(1, 128), w_bias.T)
    recv = lax.all_to_all(
        packed.reshape(NG * NB, HALF + HEADS, TB, 128), AXES, split_axis=0, concat_axis=0, tiled=True
    ).reshape(packed.shape)
    other = lax.ppermute(recv[:, :, :HALF], "c", [(0, 1), (1, 0)])
    update = attend(
        recv, other, mask.reshape(8, 128), w_key, w_value, w_query, w_gate,
        gate_bias.reshape(1, 128), w_out, out_bias.reshape(1, 128),
    )
    home = lax.all_to_all(update, GROUP, split_axis=0, concat_axis=0, tiled=True)
    return jnp.transpose(home, (1, 0, 2, 3)).reshape(8, 128, 128)


def solution(mesh):
    fine = Mesh(mesh.devices.reshape(SIZES), AXES)
    whole = P(AXES, None, None)
    placed = (whole, P(("x", "zl"), ("zh", "y", "c"), None)) + (P(),) * 10
    return jax.shard_map(
        per_device, mesh=fine, in_specs=placed, out_specs=whole, check_vma=False
    )
```

time: 89.4 us -> 81.4 us (0.911)
  Pallas kernels: 27.7 us -> 22.3 us
  local copies, waits for them, and re-layouts: 4.12 us -> 1.86 us
  other arithmetic: 1.25 us -> 0 us
  waiting for transfers between devices: 1.6 us -> 2.65 us
    pallas_call x2, Pallas kernels: 27.7 us -> 22.3 us  [the longest x1 15 us: attend(): pl.pallas_call(attend_kernel, grid=(COLS + 1,), in_specs=[pl.BlockSpec(co...]
    pad x1 -> x0, local copies, waits for them, and re-layouts: 1.26 us -> none  [per_device(): wb = jnp.pad(w_bias.T, ((0, 8 - HEADS), (0, 0)))]
    ppermute x1, waiting for transfers between devices: 1.6 us -> 2.65 us  [per_device(): other = lax.ppermute(recv[:, :, :HALF], 'c', [(0, 1), (1, 0)])]
    slice x1, local copies, waits for them, and re-layouts: 1.1 us -> 0.11 us  [per_device(): other = lax.ppermute(recv[:, :, :HALF], 'c', [(0, 1), (1, 0)])]
  transfers between devices with their start and end apart: 1 -> 1, of which waited for: 1 -> 1; matrix products, arithmetic and copies ran while one was open for 1% -> 0% of each run, Pallas kernels for 0% -> 0%
where the time goes in v2:
time: 81.4 us; the launch traced here: 81.1 us
  blocking collectives  54.2 us (67%)
  Pallas kernels  22.3 us (27%)
  waiting for transfers between devices  2.65 us (3%)
  local copies, waits for them, and re-layouts  1.86 us (2%)
    all_to_all x1, blocking collectives, per_device(): lax.all_to_all(packed.reshape(NG * NB, HALF + HEADS, TB, 128), AXES, spli...  41.4 us
    pallas_call x1, Pallas kernels, attend(): pl.pallas_call(attend_kernel, grid=(COLS + 1,), in_specs=[pl.BlockSpec(co...  15 us
    all_to_all x1, blocking collectives, per_device(): lax.all_to_all(update, GROUP, split_axis=0, concat_axis=0, tiled=True)  12.8 us
    pallas_call x1, Pallas kernels, pack(): pl.pallas_call(pack_kernel, in_specs=[VMEM, ANY, VMEM, VMEM], out_specs=A...  7.3 us
    ppermute x1, waiting for transfers between devices, per_device(): other = lax.ppermute(recv[:, :, :HALF], 'c', [(0, 1), (1, 0)])  2.65 us
  transfers between devices with their start and end apart: 1, of which 1 were waited for; matrix products, arithmetic and copies ran while one was open for 0% of the time, Pallas kernels for 0%

profile of v2, /device:TPU:0, one launch (start us, length us, event | category | flops | bytes accessed | tf_op | source)
XLA Modules:
  0.0 81.1 jit_solution(9818956450588095027)
XLA Ops:
  0.0 7.3 %pack.1 = bf16[16,8,8,8,128]{4,3,2,1,0:T(8,128)(2,1)} custom-call(bf16[8,128,128]{2,1,0:T(8,128)(2,1)} %slab_ref.1, bf16[128,64,128]{2,1,0:T(8,128)(2,1)} %pair_ref.1, f32[1,128]{1,0:T(1,128)} %bitcast.18, bf16[4,128]{1,0:T(4,128)(2,1)} %bitcast.17), custom_call_target="tpu_custom_call" | custom-call | tf_op jit(solution)/shard_map/pack/pallas_call | solution.py:83
  7.3 41.4 %all_to_all.10 = bf16[128,8,8,128]{3,2,1,0:T(8,128)(2,1)S(1)} all-to-all(bf16[128,8,8,128]{3,2,1,0:T(8,128)(2,1)} %bitcast.15), channel_id=1, replica_groups=mesh['x'=4,'zl'=2,'zh'=2,'y'=4,'c'=2] {'x','zl','zh','y','c'}, dimensions={0} | all-to-all | bytes 4194304 | tf_op jit(solution)/shard_map/all_to_all | solution.py:249
  48.7 0.0 copy-start
  48.7 0.1 slice.4
  48.8 0.1 collective-permute-start
  48.9 2.6 %collective-permute-done.other_ref = bf16[16,8,4,8,128]{4,3,2,1,0:T(8,128)(2,1)S(1)} collective-permute-done((bf16[16,8,4,8,128]{4,3,2,1,0:T(8,128)(2,1)S(1)}, bf16[16,8,4,8,128]{4,3,2,1,0:T(8,128)(2,1)S(1)}, u32[]{:S(2)}, u32[]{:S(2)}) %collective-permute-start) | collective-permute-done | bytes 1048608 | tf_op jit(solution)/shard_map/ppermute | solution.py:252
  51.6 0.0 copy-start.1
  51.6 0.0 copy-done
  51.6 1.0 %copy-done.1 = bf16[16,8,4,8,128]{4,3,2,1,0:T(8,128)(2,1)} copy-done((bf16[16,8,4,8,128]{4,3,2,1,0:T(8,128)(2,1)}, bf16[16,8,4,8,128]{4,3,2,1,0:T(8,128)(2,1)S(1)}, u32[]{:S(2)}) %copy-start.1) | copy-done | bytes 1048600
  52.6 15.0 %attend.1 = bf16[16,8,8,128]{3,2,1,0:T(8,128)(2,1)} custom-call(bf16[16,8,8,8,128]{4,3,2,1,0:T(8,128)(2,1)} %bitcast.13, bf16[16,8,4,8,128]{4,3,2,1,0:T(8,128)(2,1)} %copy-done.1, bf16[16,8,8,8,128]{4,3,2,1,0:T(8,128)(2,1)} %bitcast.14, s32[8,128]{1,0:T(8,128)} %bitcast.16, bf16[128,128]{1,0:T(8,128)(2,1)} %wk_ref.1, bf16[128,128]{1,0:T(8,128)(2,1)} %wv_ref.1, ...), custom_call_target="tpu_custom_call" | custom-call | tf_op jit(solution)/shard_map/attend/pallas_call | solution.py:210
  67.5 12.8 %all_to_all.11 = bf16[16,8,8,128]{3,2,1,0:T(8,128)(2,1)S(1)} all-to-all(bf16[16,8,8,128]{3,2,1,0:T(8,128)(2,1)} %attend.1), channel_id=1, replica_groups=mesh['x'=4,'zl'=2,'zh'=2,'y'=4,'c'=2] {'x','zl','zh'}, dimensions={0} | all-to-all | bytes 524288 | tf_op jit(solution)/shard_map/all_to_all | solution.py:257
  80.4 0.8 copy_bitcast_fusion
Async XLA Ops:
  48.7 2.9 %copy-start = (bf16[128,8,8,128]{3,2,1,0:T(8,128)(2,1)}, bf16[128,8,8,128]{3,2,1,0:T(8,128)(2,1)S(1)}, u32[]{:S(2)}) copy-start(bf16[128,8,8,128]{3,2,1,0:T(8,128)(2,1)S(1)} %all_to_all.10) | copy-start | bytes 6291460
  48.8 2.7 %collective-permute-start = (bf16[16,8,4,8,128]{4,3,2,1,0:T(8,128)(2,1)S(1)}, bf16[16,8,4,8,128]{4,3,2,1,0:T(8,128)(2,1)S(1)}, u32[]{:S(2)}, u32[]{:S(2)}) collective-permute-start(bf16[16,8,4,8,128]{4,3,2,1,0:T(8,128)(2,1)S(1)} %slice.4), channel_id=1, source_target_pairs={{0,1},{1,0},{2,3},{3,2},{4,5},{5,4},{6,7},{7,6},{8,9},{9,8},{10,11... | collective-permute-start | bytes 3145736 | tf_op jit(solution)/shard_map/ppermute | solution.py:252
  51.6 1.0 %copy-start.1 = (bf16[16,8,4,8,128]{4,3,2,1,0:T(8,128)(2,1)}, bf16[16,8,4,8,128]{4,3,2,1,0:T(8,128)(2,1)S(1)}, u32[]{:S(2)}) copy-start(bf16[16,8,4,8,128]{4,3,2,1,0:T(8,128)(2,1)S(1)} %collective-permute-done.other_ref) | copy-start | bytes 3145732

commit v3 on v2

--- a/solution.py
+++ b/solution.py
@@ -24,38 +24,33 @@
 CHUNK = 16
 
 VMEM = pl.BlockSpec(memory_space=pltpu.VMEM)
-ANY = pl.BlockSpec(memory_space=pl.ANY)
+HBM = pl.BlockSpec(memory_space=pltpu.HBM)
 
 
 def pack_kernel(
-    slab_ref, pair_ref, gain_ref, wb_ref,
-    out_ref, pbuf, nslab, npair, rows, pslab, pbias, in_sem, slab_sem, bias_sem,
+    slab_ref, pair_ref, gain_hbm, wb_hbm, out_ref, pbuf, sbuf, gain_ref, wb_ref, nslab, npair, rows, in_sem
 ):
     loads = [
         pltpu.make_async_copy(pair_ref.at[pl.ds(16 * n, 16)], pbuf.at[pl.ds(16 * n, 16)], in_sem.at[n])
         for n in range(8)
     ]
+    gain_load = pltpu.make_async_copy(gain_hbm, gain_ref, in_sem.at[8])
+    wb_load = pltpu.make_async_copy(wb_hbm, wb_ref, in_sem.at[9])
+    slab_load = pltpu.make_async_copy(slab_ref, sbuf, in_sem.at[10])
+    gain_load.start()
     for load in loads:
         load.start()
+    wb_load.start()
+    slab_load.start()
+    gain_load.wait()
     ones = jnp.full((128, 128), 1.0 / 128, BF16)
     gain = gain_ref[...]
-    wb = wb_ref[...]
 
     def norm(x):
         d = x.astype(F32) - jnp.dot(x, ones, preferred_element_type=F32)
         spread = jnp.mean(d * d, axis=-1, keepdims=True)
         return d * lax.rsqrt(spread + 1e-5) * gain
 
-    nslab[...] = norm(slab_ref[...].reshape(1024, 128))
-    for col in range(128):
-        piece = nslab[pl.ds(col, TB, stride=128), :].astype(BF16)
-        pslab[col // COLS, col % COLS // HALF, col % HALF] = piece
-    stores = [
-        pltpu.make_async_copy(pslab, out_ref.at[:, pl.ds(2 * y, 2), pl.ds(0, HALF)], slab_sem.at[y])
-        for y in range(4)
-    ]
-    for store in stores:
-        store.start()
     for n in range(8):
         loads[n].wait()
         x = norm(pbuf[16 * n : 16 * n + 16].reshape(1024, 128))
@@ -63,45 +58,48 @@
             for b in range(NB):
                 at = 1024 * b + TB * (16 * n + k)
                 npair[at : at + TB, :] = x[64 * k + TB * b : 64 * k + TB * b + TB]
+    wb_load.wait()
+    wb = wb_ref[...]
+    slab_load.wait()
+    nslab[...] = norm(sbuf[...].reshape(1024, 128))
     for b in range(NB):
         for i in range(TB):
             x = npair[pl.ds(1024 * b + i, 128, stride=TB), :].astype(BF16)
             t = lax.dot_general(wb, x, (((1,), (1,)), ((), ())), preferred_element_type=F32)
             rows[pl.ds(HEADS * TB * b + i, HEADS, stride=TB), :] = t
-    pbias[...] = rows[...].reshape(NB, HEADS, TB, 128).astype(BF16)
-    more = [
-        pltpu.make_async_copy(pbias, out_ref.at[g, :, pl.ds(HALF, HEADS)], bias_sem.at[g])
-        for g in range(NG)
-    ]
-    for store in more:
-        store.start()
-    for store in stores + more:
-        store.wait()
+        at = slice(HEADS * TB * b, HEADS * TB * b + HEADS * TB)
+        bias = rows[at, :].reshape(HEADS, TB, 128).astype(BF16)
+        for g in range(NG):
+            out_ref[g, b, HALF : HALF + HEADS] = bias
+    for col in range(128):
+        piece = nslab[pl.ds(col, TB, stride=128), :].astype(BF16)
+        for y in range(4):
+            out_ref[col // COLS, 2 * y + col % COLS // HALF, col % HALF] = piece
 
 
 def pack(slab, pair, gain, wb):
     return pl.pallas_call(
         pack_kernel,
-        in_specs=[VMEM, ANY, VMEM, VMEM],
-        out_specs=ANY,
+        in_specs=[HBM] * 4,
+        out_specs=VMEM,
         out_shape=jax.ShapeDtypeStruct((NG, NB, HALF + HEADS, TB, 128), BF16),
         scratch_shapes=[
             pltpu.VMEM((128, 64, 128), BF16),
+            pltpu.VMEM((8, 128, 128), BF16),
+            pltpu.VMEM((1, 128), F32),
+            pltpu.VMEM((HEADS, 128), BF16),
             pltpu.VMEM((1024, 128), F32),
             pltpu.VMEM((8192, 128), F32),
-            pltpu.VMEM((NB * HEADS * TB, 128), F32),
-            pltpu.VMEM((NG, 2, HALF, TB, 128), BF16),
-            pltpu.VMEM((NB, HEADS, TB, 128), BF16),
-            pltpu.SemaphoreType.DMA((8,)),
-            pltpu.SemaphoreType.DMA((4,)),
-            pltpu.SemaphoreType.DMA((NG,)),
+            pltpu.VMEM((NB * HEADS * TB + 64, 128), F32),
+            pltpu.SemaphoreType.DMA((11,)),
         ],
+        compiler_params=pltpu.CompilerParams(vmem_limit_bytes=30 << 20),
         name="pack",
-    )(slab, pair, gain, wb)
+    )(*(pltpu.with_memory_space_constraint(a, pltpu.HBM) for a in (slab, pair, gain, wb)))
 
 
 def attend_kernel(
-    own_ref, other_ref, tiles_ref, mask_ref, wk_ref, wv_ref, wq_ref, wg_ref, gb_ref, wo_ref, ob_ref,
+    recv_ref, other_ref, mask_ref, wk_ref, wv_ref, wq_ref, wg_ref, gb_ref, wo_ref, ob_ref,
     out_ref, bias, s_even, s_odd, v_even, v_odd, g_even, g_odd, weights, inverse, product, upd,
 ):
     step = pl.program_id(0)
@@ -113,17 +111,19 @@
         for r in range(8):
             shift = (mask_ref[r : r + 1, :].astype(F32) - 1.0) * 1e9
             for h in range(HEADS):
-                tile = tiles_ref[2 * r : 2 * r + 2, :, h].astype(F32).reshape(128, 128)
+                tile = recv_ref[2 * r : 2 * r + 2, :, HALF + h].astype(F32).reshape(128, 128)
                 bias[h * 128 : (h + 1) * 128, r * 128 : (r + 1) * 128] = (tile + shift) * LOG2E
 
     lane_head = lax.broadcasted_iota(jnp.int32, (128, 128), 1) // 32
     mine = step < HALF
+    j_own = jnp.minimum(step, HALF - 1)
+    j_other = jnp.clip(step - HALF, 0, HALF - 1)
 
     def pick(own, other):
         return jnp.where(mine, own.astype(F32), other.astype(F32))
 
     def queries(gate):
-        xq = pick(own_ref[:, b, 0], other_ref[:, b, 0]).reshape(128, 128).astype(BF16)
+        xq = pick(recv_ref[:, b, j_own], other_ref[:, b, j_other]).reshape(128, 128).astype(BF16)
         wqg = jnp.concatenate([wq_ref[...], wg_ref[...]], axis=1)
         qg = jnp.dot(xq, wqg, preferred_element_type=F32)
         gate[...] = jax.nn.sigmoid(qg[:, 128:] + gb_ref[...])
@@ -135,7 +135,7 @@
     def scores(n, q, new, value):
         at = slice(n * 4, n * 4 + 4)
         keys = slice(n * 256, n * 256 + 256)
-        x = pick(own_ref[at, :, 0], other_ref[at, :, 0]).reshape(256, 128).astype(BF16)
+        x = pick(recv_ref[at, :, j_own], other_ref[at, :, j_other]).reshape(256, 128).astype(BF16)
         wkv = jnp.concatenate([wk_ref[...], wv_ref[...]], axis=1)
         kv = jnp.dot(x, wkv, preferred_element_type=F32)
         value[keys, :] = kv[:, 128:].astype(BF16)
@@ -211,9 +211,8 @@
         attend_kernel,
         grid=(COLS + 1,),
         in_specs=[
-            pl.BlockSpec(column, lambda s: (0, 0, jnp.minimum(s, HALF - 1), 0, 0)),
-            pl.BlockSpec(column, lambda s: (0, 0, jnp.clip(s - HALF, 0, HALF - 1), 0, 0)),
-            pl.BlockSpec((NG, NB, HEADS, TB, 128), lambda s: (0, 0, 1, 0, 0)),
+            VMEM,
+            VMEM,
             pl.BlockSpec((8, 128), const),
             square,
             square,
@@ -238,8 +237,12 @@
             pltpu.VMEM((512, 128), F32),
             pltpu.VMEM((1024, 128), F32),
         ],
+        compiler_params=pltpu.CompilerParams(vmem_limit_bytes=40 << 20),
         name="attend",
-    )(recv, other, recv, mask, wk, wv, wq, wg, gb, wo, ob)
+    )(
+        pltpu.with_memory_space_constraint(recv, pltpu.VMEM),
+        pltpu.with_memory_space_constraint(other, pltpu.VMEM),
+        mask, wk, wv, wq, wg, gb, wo, ob)
 
 
 def per_device(

time: 81.4 us -> 75.8 us (0.931)
  Pallas kernels: 22.3 us -> 18.3 us
  local copies, waits for them, and re-layouts: 1.86 us -> 0.9 us
    pallas_call x2, Pallas kernels: 22.3 us -> 18.3 us  [the longest x1 12.5 us: attend(): pl.pallas_call(attend_kernel, grid=(COLS + 1,), in_specs=[VMEM, VMEM, pl....]
    unnamed x4 -> x16, local copies, waits for them, and re-layouts: 1 us -> 0.04 us
where the time goes in v3:
time: 75.8 us; the launch traced here: 75.7 us
  blocking collectives  53.7 us (71%)
  Pallas kernels  18.3 us (24%)
  waiting for transfers between devices  2.65 us (3%)
  local copies, waits for them, and re-layouts  0.9 us (1%)
    all_to_all x1, blocking collectives, per_device(): lax.all_to_all(packed.reshape(NG * NB, HALF + HEADS, TB, 128), AXES, spli...  41.2 us
    all_to_all x1, blocking collectives, per_device(): lax.all_to_all(update, GROUP, split_axis=0, concat_axis=0, tiled=True)  12.5 us
    pallas_call x1, Pallas kernels, attend(): pl.pallas_call(attend_kernel, grid=(COLS + 1,), in_specs=[VMEM, VMEM, pl....  12.5 us
    pallas_call x1, Pallas kernels, pack(): pl.pallas_call(pack_kernel, in_specs=[HBM] * 4, out_specs=VMEM, out_shape...  5.8 us
    ppermute x1, waiting for transfers between devices, per_device(): other = lax.ppermute(recv[:, :, :HALF], 'c', [(0, 1), (1, 0)])  2.65 us
  transfers between devices with their start and end apart: 1, of which 1 were waited for; matrix products, arithmetic and copies ran while one was open for 0% of the time, Pallas kernels for 0%

profile of v3, /device:TPU:0, one launch (start us, length us, event | category | flops | bytes accessed | tf_op | source)
XLA Modules:
  0.0 75.7 jit_solution(468727596642727466)
XLA Ops:
  0.0 5.8 %pack.1 = bf16[16,8,8,8,128]{4,3,2,1,0:T(8,128)(2,1)S(1)} custom-call(bf16[8,128,128]{2,1,0:T(8,128)(2,1)} %slab_ref.1, bf16[128,64,128]{2,1,0:T(8,128)(2,1)} %pair_ref.1, f32[1,128]{1,0:T(1,128)} %bitcast.19, bf16[4,128]{1,0:T(4,128)(2,1)} %bitcast.18), custom_call_target="tpu_custom_call" | custom-call | tf_op jit(solution)/shard_map/pack/pallas_call | solution.py:81
  5.8 41.2 %all_to_all.10 = bf16[128,8,8,128]{3,2,1,0:T(8,128)(2,1)S(1)} all-to-all(bf16[128,8,8,128]{3,2,1,0:T(8,128)(2,1)S(1)} %bitcast.14), channel_id=1, replica_groups=mesh['x'=4,'zl'=2,'zh'=2,'y'=4,'c'=2] {'x','zl','zh','y','c'}, dimensions={0} | all-to-all | bytes 4194304 | tf_op jit(solution)/shard_map/all_to_all | solution.py:252
  47.0 0.0 copy-start
  47.0 0.0 copy-start.1
  47.0 0.0 copy-start.2
  47.0 0.0 copy-start.3
  47.0 0.0 copy-start.4
  47.0 0.0 copy-start.5
  47.0 0.0 copy-start.6
  47.0 0.0 copy-start.7
  47.1 0.1 slice.4
  47.2 0.1 collective-permute-start
  47.3 2.6 %collective-permute-done.other_ref = bf16[16,8,4,8,128]{4,3,2,1,0:T(8,128)(2,1)S(1)} collective-permute-done((bf16[16,8,4,8,128]{4,3,2,1,0:T(8,128)(2,1)S(1)}, bf16[16,8,4,8,128]{4,3,2,1,0:T(8,128)(2,1)S(1)}, u32[]{:S(2)}, u32[]{:S(2)}) %collective-permute-start) | collective-permute-done | bytes 1048608 | tf_op jit(solution)/shard_map/ppermute | solution.py:255
  49.9 0.0 copy-done
  49.9 0.0 copy-done.1
  49.9 0.0 copy-done.2
  49.9 0.0 copy-done.3
  49.9 0.0 copy-done.4
  49.9 0.0 copy-done.5
  50.0 0.0 copy-done.6
  50.0 0.0 copy-done.7
  50.0 12.5 %attend.1 = bf16[16,8,8,128]{3,2,1,0:T(8,128)(2,1)S(1)} custom-call(bf16[16,8,8,8,128]{4,3,2,1,0:T(8,128)(2,1)S(1)} %bitcast.13, bf16[16,8,4,8,128]{4,3,2,1,0:T(8,128)(2,1)S(1)} %collective-permute-done.other_ref, s32[8,128]{1,0:T(8,128)S(1)} %bitcast.15, bf16[128,128]{1,0:T(8,128)(2,1)S(1)} %copy-done, bf16[128,128]{1,0:T(8,128)(2,1)S(1)} %copy-done.1, ...), custom_call_target="tpu_custom_call" | custom-call | tf_op jit(solution)/shard_map/attend/pallas_call | solution.py:210
  62.4 12.5 %all_to_all.11 = bf16[16,8,8,128]{3,2,1,0:T(8,128)(2,1)S(1)} all-to-all(bf16[16,8,8,128]{3,2,1,0:T(8,128)(2,1)S(1)} %attend.1), channel_id=1, replica_groups=mesh['x'=4,'zl'=2,'zh'=2,'y'=4,'c'=2] {'x','zl','zh'}, dimensions={0} | all-to-all | bytes 524288 | tf_op jit(solution)/shard_map/all_to_all | solution.py:260
  74.9 0.8 copy_bitcast_fusion
Async XLA Ops:
  47.0 2.9 %copy-start = (bf16[128,128]{1,0:T(8,128)(2,1)S(1)}, bf16[128,128]{1,0:T(8,128)(2,1)}, u32[]{:S(2)}) copy-start(bf16[128,128]{1,0:T(8,128)(2,1)} %wk_ref.1) | copy-start | bytes 98308
  47.0 2.9 %copy-start.1 = (bf16[128,128]{1,0:T(8,128)(2,1)S(1)}, bf16[128,128]{1,0:T(8,128)(2,1)}, u32[]{:S(2)}) copy-start(bf16[128,128]{1,0:T(8,128)(2,1)} %wv_ref.1) | copy-start | bytes 98308
  47.0 2.9 %copy-start.2 = (bf16[128,128]{1,0:T(8,128)(2,1)S(1)}, bf16[128,128]{1,0:T(8,128)(2,1)}, u32[]{:S(2)}) copy-start(bf16[128,128]{1,0:T(8,128)(2,1)} %wq_ref.1) | copy-start | bytes 98308
  47.0 2.9 %copy-start.3 = (bf16[128,128]{1,0:T(8,128)(2,1)S(1)}, bf16[128,128]{1,0:T(8,128)(2,1)}, u32[]{:S(2)}) copy-start(bf16[128,128]{1,0:T(8,128)(2,1)} %wg_ref.1) | copy-start | bytes 98308
  47.0 2.9 %copy-start.4 = (bf16[128,128]{1,0:T(8,128)(2,1)S(1)}, bf16[128,128]{1,0:T(8,128)(2,1)}, u32[]{:S(2)}) copy-start(bf16[128,128]{1,0:T(8,128)(2,1)} %wo_ref.1) | copy-start | bytes 98308
  47.0 2.9 %copy-start.5 = (s32[1024]{0:T(1024)S(1)}, s32[1024]{0:T(1024)}, u32[]{:S(2)}) copy-start(s32[1024]{0:T(1024)} %param.14) | copy-start | bytes 12292
  47.0 2.9 %copy-start.6 = (f32[128]{0:T(128)S(1)}, f32[128]{0:T(128)}, u32[]{:S(2)}) copy-start(f32[128]{0:T(128)} %param.20) | copy-start | bytes 1540
  47.0 2.9 %copy-start.7 = (f32[128]{0:T(128)S(1)}, f32[128]{0:T(128)}, u32[]{:S(2)}) copy-start(f32[128]{0:T(128)} %param.23) | copy-start | bytes 1540
  47.2 2.7 %collective-permute-start = (bf16[16,8,4,8,128]{4,3,2,1,0:T(8,128)(2,1)S(1)}, bf16[16,8,4,8,128]{4,3,2,1,0:T(8,128)(2,1)S(1)}, u32[]{:S(2)}, u32[]{:S(2)}) collective-permute-start(bf16[16,8,4,8,128]{4,3,2,1,0:T(8,128)(2,1)S(1)} %slice.4), channel_id=1, source_target_pairs={{0,1},{1,0},{2,3},{3,2},{4,5},{5,4},{6,7},{7,6},{8,9},{9,8},{10,11... | collective-permute-start | bytes 3145736 | tf_op jit(solution)/shard_map/ppermute | solution.py:255

commit v4 on v3

--- a/solution.py
+++ b/solution.py
@@ -100,7 +100,7 @@
 
 def attend_kernel(
     recv_ref, other_ref, mask_ref, wk_ref, wv_ref, wq_ref, wg_ref, gb_ref, wo_ref, ob_ref,
-    out_ref, bias, s_even, s_odd, v_even, v_odd, g_even, g_odd, weights, inverse, product, upd,
+    out_ref, bias, s_even, s_odd, v_even, v_odd, g_even, g_odd, weights, product, upd,
 ):
     step = pl.program_id(0)
     core = lax.axis_index("c")
@@ -115,15 +115,10 @@
                 bias[h * 128 : (h + 1) * 128, r * 128 : (r + 1) * 128] = (tile + shift) * LOG2E
 
     lane_head = lax.broadcasted_iota(jnp.int32, (128, 128), 1) // 32
-    mine = step < HALF
-    j_own = jnp.minimum(step, HALF - 1)
-    j_other = jnp.clip(step - HALF, 0, HALF - 1)
-
-    def pick(own, other):
-        return jnp.where(mine, own.astype(F32), other.astype(F32))
-
-    def queries(gate):
-        xq = pick(recv_ref[:, b, j_own], other_ref[:, b, j_other]).reshape(128, 128).astype(BF16)
+
+    def queries(source, gate):
+        ref, j = source
+        xq = ref[:, b, j].astype(F32).reshape(128, 128).astype(BF16)
         wqg = jnp.concatenate([wq_ref[...], wg_ref[...]], axis=1)
         qg = jnp.dot(xq, wqg, preferred_element_type=F32)
         gate[...] = jax.nn.sigmoid(qg[:, 128:] + gb_ref[...])
@@ -132,13 +127,14 @@
             [jnp.where(lane_head == h, q, 0.0).astype(BF16) for h in range(HEADS)], axis=0
         )
 
-    def scores(n, q, new, value):
+    def scores(n, source, q, new, value):
+        ref, j = source
         at = slice(n * 4, n * 4 + 4)
         keys = slice(n * 256, n * 256 + 256)
-        x = pick(recv_ref[at, :, j_own], other_ref[at, :, j_other]).reshape(256, 128).astype(BF16)
+        x = ref[at, :, j].astype(F32).reshape(256, 128).astype(BF16)
         wkv = jnp.concatenate([wk_ref[...], wv_ref[...]], axis=1)
         kv = jnp.dot(x, wkv, preferred_element_type=F32)
-        value[keys, :] = kv[:, 128:].astype(BF16)
+        value[keys, :128] = kv[:, 128:].astype(BF16)
         s = lax.dot_general(
             q, kv[:, :128].astype(BF16), (((1,), (1,)), ((), ())), preferred_element_type=F32
         )
@@ -149,14 +145,12 @@
             at = slice(m, m + CHUNK)
             s = old[at, :]
             p = jnp.exp2(s - jnp.max(s, axis=-1, keepdims=True))
-            total = jnp.sum(p, axis=-1, keepdims=True)
             weights[at, :] = p.astype(BF16)
-            inverse[at, :] = jnp.broadcast_to(1.0 / total, (CHUNK, 128))
 
     def products(n, value):
         at = slice(n * 256, n * 256 + 256)
         o = jnp.dot(weights[at, :], value[...], preferred_element_type=F32)
-        product[at, :] = o * inverse[at, :]
+        product[at, :] = o[:, :128] * (1.0 / o[:, 128:])
 
     def finish(gate):
         att = product[0:128]
@@ -168,12 +162,12 @@
         col = jnp.where(before < HALF, before + core * HALF, before - core * HALF)
         upd[pl.ds(col, 128, stride=COLS), :] = u
 
-    def body(new, old):
+    def body(source, new, old):
         if new is not None:
-            q = queries(new[2])
+            q = queries(source, new[2])
         for n in range(4):
             if new is not None:
-                scores(n, q, new[0], new[1])
+                scores(n, source, q, new[0], new[1])
             if old is not None:
                 softmax(n, old[0])
                 if n % 2:
@@ -186,19 +180,25 @@
 
     @pl.when(step == 0)
     def _():
-        body(even, None)
-
-    @pl.when((step % 2 == 0) & (step > 0) & (step < COLS))
-    def _():
-        body(even, odd)
-
-    @pl.when(step % 2 == 1)
-    def _():
-        body(odd, even)
+        v_even[:, 128:] = jnp.ones((1024, 128), BF16)
+        v_odd[:, 128:] = jnp.ones((1024, 128), BF16)
+        body((recv_ref, 0), even, None)
+
+    own = (recv_ref, jnp.minimum(step, HALF - 1))
+    other = (other_ref, jnp.clip(step - HALF, 0, HALF - 1))
+    for source, here in ((own, (step > 0) & (step < HALF)), (other, (step >= HALF) & (step < COLS))):
+
+        @pl.when(here & (step % 2 == 0))
+        def _(source=source):
+            body(source, even, odd)
+
+        @pl.when(here & (step % 2 == 1))
+        def _(source=source):
+            body(source, odd, even)
 
     @pl.when(step == COLS)
     def _():
-        body(None, odd)
+        body(None, None, odd)
         out_ref[...] = upd[...].reshape(16, TB, COLS, 128).astype(BF16)
 
 
@@ -228,12 +228,11 @@
             pltpu.VMEM((512, 1024), F32),
             pltpu.VMEM((512, 1024), F32),
             pltpu.VMEM((512, 1024), F32),
-            pltpu.VMEM((1024, 128), BF16),
-            pltpu.VMEM((1024, 128), BF16),
+            pltpu.VMEM((1024, 256), BF16),
+            pltpu.VMEM((1024, 256), BF16),
             pltpu.VMEM((128, 128), F32),
             pltpu.VMEM((128, 128), F32),
             pltpu.VMEM((512, 1024), BF16),
-            pltpu.VMEM((512, 128), F32),
             pltpu.VMEM((512, 128), F32),
             pltpu.VMEM((1024, 128), F32),
         ],

time: 75.8 us -> 74.8 us (0.987)
  Pallas kernels: 18.3 us -> 17.2 us
    pallas_call x1, Pallas kernels: 12.5 us -> 11.4 us  [attend(): pl.pallas_call(attend_kernel, grid=(COLS + 1,), in_specs=[VMEM, VMEM, pl....]
where the time goes in v4:
time: 74.8 us; the launch traced here: 74.6 us
  blocking collectives  53.7 us (72%)
  Pallas kernels  17.2 us (23%)
  waiting for transfers between devices  2.65 us (4%)
  local copies, waits for them, and re-layouts  0.9 us (1%)
    all_to_all x1, blocking collectives, per_device(): lax.all_to_all(packed.reshape(NG * NB, HALF + HEADS, TB, 128), AXES, spli...  41.2 us
    all_to_all x1, blocking collectives, per_device(): lax.all_to_all(update, GROUP, split_axis=0, concat_axis=0, tiled=True)  12.5 us
    pallas_call x1, Pallas kernels, attend(): pl.pallas_call(attend_kernel, grid=(COLS + 1,), in_specs=[VMEM, VMEM, pl....  11.4 us
    pallas_call x1, Pallas kernels, pack(): pl.pallas_call(pack_kernel, in_specs=[HBM] * 4, out_specs=VMEM, out_shape...  5.8 us
    ppermute x1, waiting for transfers between devices, per_device(): other = lax.ppermute(recv[:, :, :HALF], 'c', [(0, 1), (1, 0)])  2.65 us
  transfers between devices with their start and end apart: 1, of which 1 were waited for; matrix products, arithmetic and copies ran while one was open for 0% of the time, Pallas kernels for 0%

profile of v4, /device:TPU:0, one launch (start us, length us, event | category | flops | bytes accessed | tf_op | source)
XLA Modules:
  0.0 74.6 jit_solution(9474446645470347827)
XLA Ops:
  0.0 5.8 %pack.1 = bf16[16,8,8,8,128]{4,3,2,1,0:T(8,128)(2,1)S(1)} custom-call(bf16[8,128,128]{2,1,0:T(8,128)(2,1)} %slab_ref.1, bf16[128,64,128]{2,1,0:T(8,128)(2,1)} %pair_ref.1, f32[1,128]{1,0:T(1,128)} %bitcast.19, bf16[4,128]{1,0:T(4,128)(2,1)} %bitcast.18), custom_call_target="tpu_custom_call" | custom-call | tf_op jit(solution)/shard_map/pack/pallas_call | solution.py:81
  5.8 41.2 %all_to_all.10 = bf16[128,8,8,128]{3,2,1,0:T(8,128)(2,1)S(1)} all-to-all(bf16[128,8,8,128]{3,2,1,0:T(8,128)(2,1)S(1)} %bitcast.14), channel_id=1, replica_groups=mesh['x'=4,'zl'=2,'zh'=2,'y'=4,'c'=2] {'x','zl','zh','y','c'}, dimensions={0} | all-to-all | bytes 4194304 | tf_op jit(solution)/shard_map/all_to_all | solution.py:251
  47.0 0.0 copy-start
  47.0 0.0 copy-start.1
  47.0 0.0 copy-start.2
  47.0 0.0 copy-start.3
  47.0 0.0 copy-start.4
  47.0 0.0 copy-start.5
  47.0 0.0 copy-start.6
  47.0 0.0 copy-start.7
  47.1 0.1 slice.4
  47.2 0.1 collective-permute-start
  47.3 2.6 %collective-permute-done.other_ref = bf16[16,8,4,8,128]{4,3,2,1,0:T(8,128)(2,1)S(1)} collective-permute-done((bf16[16,8,4,8,128]{4,3,2,1,0:T(8,128)(2,1)S(1)}, bf16[16,8,4,8,128]{4,3,2,1,0:T(8,128)(2,1)S(1)}, u32[]{:S(2)}, u32[]{:S(2)}) %collective-permute-start) | collective-permute-done | bytes 1048608 | tf_op jit(solution)/shard_map/ppermute | solution.py:254
  49.9 0.0 copy-done
  49.9 0.0 copy-done.1
  49.9 0.0 copy-done.2
  49.9 0.0 copy-done.3
  49.9 0.0 copy-done.4
  49.9 0.0 copy-done.5
  50.0 0.0 copy-done.6
  50.0 0.0 copy-done.7
  50.0 11.4 %attend.1 = bf16[16,8,8,128]{3,2,1,0:T(8,128)(2,1)S(1)} custom-call(bf16[16,8,8,8,128]{4,3,2,1,0:T(8,128)(2,1)S(1)} %bitcast.13, bf16[16,8,4,8,128]{4,3,2,1,0:T(8,128)(2,1)S(1)} %collective-permute-done.other_ref, s32[8,128]{1,0:T(8,128)S(1)} %bitcast.15, bf16[128,128]{1,0:T(8,128)(2,1)S(1)} %copy-done, bf16[128,128]{1,0:T(8,128)(2,1)S(1)} %copy-done.1, ...), custom_call_target="tpu_custom_call" | custom-call | tf_op jit(solution)/shard_map/attend/pallas_call | solution.py:210
  61.4 12.5 %all_to_all.11 = bf16[16,8,8,128]{3,2,1,0:T(8,128)(2,1)S(1)} all-to-all(bf16[16,8,8,128]{3,2,1,0:T(8,128)(2,1)S(1)} %attend.1), channel_id=1, replica_groups=mesh['x'=4,'zl'=2,'zh'=2,'y'=4,'c'=2] {'x','zl','zh'}, dimensions={0} | all-to-all | bytes 524288 | tf_op jit(solution)/shard_map/all_to_all | solution.py:259
  73.8 0.8 %copy_bitcast_fusion = bf16[8,128,128]{2,1,0:T(8,128)(2,1)} fusion(bf16[16,8,8,128]{3,2,1,0:T(8,128)(2,1)S(1)} %all_to_all.11), kind=kLoop, calls=%fused_computation | loop fusion | bytes 524288 | tf_op jit(solution)/shard_map/reshape | solution.py:260
Async XLA Ops:
  47.0 2.9 %copy-start = (bf16[128,128]{1,0:T(8,128)(2,1)S(1)}, bf16[128,128]{1,0:T(8,128)(2,1)}, u32[]{:S(2)}) copy-start(bf16[128,128]{1,0:T(8,128)(2,1)} %wk_ref.1) | copy-start | bytes 98308
  47.0 2.9 %copy-start.1 = (bf16[128,128]{1,0:T(8,128)(2,1)S(1)}, bf16[128,128]{1,0:T(8,128)(2,1)}, u32[]{:S(2)}) copy-start(bf16[128,128]{1,0:T(8,128)(2,1)} %wv_ref.1) | copy-start | bytes 98308
  47.0 2.9 %copy-start.2 = (bf16[128,128]{1,0:T(8,128)(2,1)S(1)}, bf16[128,128]{1,0:T(8,128)(2,1)}, u32[]{:S(2)}) copy-start(bf16[128,128]{1,0:T(8,128)(2,1)} %wq_ref.1) | copy-start | bytes 98308
  47.0 2.9 %copy-start.3 = (bf16[128,128]{1,0:T(8,128)(2,1)S(1)}, bf16[128,128]{1,0:T(8,128)(2,1)}, u32[]{:S(2)}) copy-start(bf16[128,128]{1,0:T(8,128)(2,1)} %wg_ref.1) | copy-start | bytes 98308
  47.0 2.9 %copy-start.4 = (bf16[128,128]{1,0:T(8,128)(2,1)S(1)}, bf16[128,128]{1,0:T(8,128)(2,1)}, u32[]{:S(2)}) copy-start(bf16[128,128]{1,0:T(8,128)(2,1)} %wo_ref.1) | copy-start | bytes 98308
  47.0 2.9 %copy-start.5 = (s32[1024]{0:T(1024)S(1)}, s32[1024]{0:T(1024)}, u32[]{:S(2)}) copy-start(s32[1024]{0:T(1024)} %param.14) | copy-start | bytes 12292
  47.0 2.9 %copy-start.6 = (f32[128]{0:T(128)S(1)}, f32[128]{0:T(128)}, u32[]{:S(2)}) copy-start(f32[128]{0:T(128)} %param.20) | copy-start | bytes 1540
  47.0 2.9 %copy-start.7 = (f32[128]{0:T(128)S(1)}, f32[128]{0:T(128)}, u32[]{:S(2)}) copy-start(f32[128]{0:T(128)} %param.23) | copy-start | bytes 1540
  47.2 2.7 %collective-permute-start = (bf16[16,8,4,8,128]{4,3,2,1,0:T(8,128)(2,1)S(1)}, bf16[16,8,4,8,128]{4,3,2,1,0:T(8,128)(2,1)S(1)}, u32[]{:S(2)}, u32[]{:S(2)}) collective-permute-start(bf16[16,8,4,8,128]{4,3,2,1,0:T(8,128)(2,1)S(1)} %slice.4), channel_id=1, source_target_pairs={{0,1},{1,0},{2,3},{3,2},{4,5},{5,4},{6,7},{7,6},{8,9},{9,8},{10,11... | collective-permute-start | bytes 3145736 | tf_op jit(solution)/shard_map/ppermute | solution.py:254
